TPU v7x, 32 devices: a whole 2x2x4 slice. The times are simulated.
32 devices in a mesh: gx: 4 (over y, core), gy: 8 (over z, x).
Axes of the slice: x: 2, y: 2, z: 4, core: 2. Of those that a mesh axis runs over, the one named last changes fastest.
Arguments:
- pixels: int32 [16, 16, 4, 131072], P('gy', 'gx'), may hold values from 0 to 255, as said below
- weights: bfloat16 [16, 16, 4, 131072], P('gy', 'gx'), may hold values from 0.25 to 1
- adjacency: int32 [2, 16, 16], replicated, may hold values 0 or 1
Outputs:
- log_gain: float32 [16, 16], P('gy', 'gx')
Inputs may be any that keep to these rules, and one draw needn't show every extreme that they name: `pixels`: bin indices of 8-bit intensities. `adjacency`: entry [0, r, c] is 1 where tile (r, c) and the tile to its right share a usable border, entry [1, r, c] likewise for the tile below; entries of pairs beyond the grid's edge are read by no output.
All inputs are finite; a program needn't handle non-finite values.
Results may differ from a plain program's by a relative error of at most 0.0003.
Values may be sent and summed in bfloat16 or wider, within the bound.
A program may use at most 128 MiB of HBM per device.

v0:
```python
import functools
import jax
import jax.numpy as jnp
from jax import lax
from jax.experimental import pallas as pl
from jax.experimental.pallas import tpu as pltpu
from jax.sharding import PartitionSpec as P

ITERS = 20
WIDTH = 16384
EDGE_WIDTH = 16384
SUBS = 4
PER_DOT = 4


anchor_weight = 0.5
mismatch_scale = 8.0


def chunk_width(length, width):
    while length % width:
        width //= 2
    return width


def one_hots(bins, joint, level, shape):
    bins16 = jnp.broadcast_to(bins, shape).astype(jnp.int16)
    upper = (bins16 & 240) == level * 16
    lower = (bins16 & 15) == level
    joint16 = jnp.broadcast_to(joint, shape).astype(jnp.bfloat16)
    zero = jnp.zeros(shape, jnp.bfloat16)
    return jnp.where(upper, joint16, zero), jnp.where(lower, jnp.ones(shape, jnp.bfloat16), zero)


def accumulate(dots, read_bins, read_joint, sums, width):
    depth = width // SUBS
    shape = (16, depth)
    level = lax.broadcasted_iota(jnp.int32, shape, 0).astype(jnp.int16)
    for index, strips in enumerate(dots):
        left, right = [], []
        for strip in strips:
            for sub in range(SUBS):
                lanes = slice(sub * depth, (sub + 1) * depth)
                first, second = one_hots(read_bins(strip, lanes), read_joint(strip, lanes), level, shape)
                left.append(first)
                right.append(second)
        left = jnp.concatenate(left, axis=0)
        right = jnp.concatenate(right, axis=0)
        counts = lax.dot_general(
            left, right, (((1,), (1,)), ((), ())), preferred_element_type=jnp.float32
        )
        sums[index] += counts


def finish(dots, sums, out_ref):
    place = 0
    for index, strips in enumerate(dots):
        for number in range(len(strips)):
            total = jnp.zeros((16, 16), jnp.float32)
            for sub in range(SUBS):
                start = (number * SUBS + sub) * 16
                total += sums[index, start : start + 16, start : start + 16]
            out_ref[place] = total
            place += 1


def group(strips):
    return [strips[i : i + PER_DOT] for i in range(0, len(strips), PER_DOT)]


def inner_strips(rows, columns):
    strips = []
    for row in range(rows - 1):
        for column in range(columns):
            strips += [(row, column, 1), (row + 1, column, 0)]
    for row in range(rows):
        for column in range(columns - 1):
            strips += [(row, column, 3), (row, column + 1, 2)]
    return strips


def outer_strips(rows, columns):
    strips = [(0, column, 0) for column in range(columns)]
    strips += [(rows - 1, column, 1) for column in range(columns)]
    strips += [(row, 0, 2) for row in range(rows)]
    strips += [(row, columns - 1, 3) for row in range(rows)]
    return strips


def partner_of(strip):
    row, column, side = strip
    return [
        (row - 1, column, 1),
        (row + 1, column, 0),
        (row, column - 1, 3),
        (row, column + 1, 2),
    ][side]


def edges_kernel(w_ref, up_ref, down_ref, left_ref, right_ref):
    rows, columns = w_ref.shape[:2]
    for column in range(columns):
        up_ref[column : column + 1] = w_ref[0, column, 0:1, :]
        down_ref[column : column + 1] = w_ref[rows - 1, column, 1:2, :]
    for row in range(rows):
        left_ref[row : row + 1] = w_ref[row, 0, 2:3, :]
        right_ref[row : row + 1] = w_ref[row, columns - 1, 3:4, :]


def edges(weights):
    rows, columns, sides, length = weights.shape
    width = chunk_width(length, EDGE_WIDTH)
    row_shape = jax.ShapeDtypeStruct((columns, length), weights.dtype)
    column_shape = jax.ShapeDtypeStruct((rows, length), weights.dtype)
    row_spec = pl.BlockSpec((columns, width), lambda i: (0, i))
    column_spec = pl.BlockSpec((rows, width), lambda i: (0, i))
    return pl.pallas_call(
        edges_kernel,
        grid=(length // width,),
        in_specs=[pl.BlockSpec((rows, columns, sides, width), lambda i: (0, 0, 0, i))],
        out_specs=[row_spec, row_spec, column_spec, column_spec],
        out_shape=[row_shape, row_shape, column_shape, column_shape],
        name="edges",
    )(weights)


def inner_kernel(dots, p_ref, w_ref, out_ref, wide, sums):
    @pl.when(pl.program_id(0) == 0)
    def _():
        sums[...] = jnp.zeros_like(sums)

    wide[...] = w_ref[...].astype(jnp.float32)

    def read_bins(strip, lanes):
        row, column, side = strip
        return p_ref[row, column, side : side + 1, lanes]

    def read_joint(strip, lanes):
        row, column, side = strip
        if side in (0, 2):
            row, column, side = partner_of(strip)
        other_row, other_column, other_side = partner_of((row, column, side))
        return (
            wide[row, column, side : side + 1, lanes]
            * wide[other_row, other_column, other_side : other_side + 1, lanes]
        )

    accumulate(dots, read_bins, read_joint, sums, p_ref.shape[-1])

    @pl.when(pl.program_id(0) == pl.num_programs(0) - 1)
    def _():
        finish(dots, sums, out_ref)


def outer_kernel(dots, p_ref, w_ref, up_ref, down_ref, left_ref, right_ref, out_ref, wide, row_wide, column_wide, sums):
    @pl.when(pl.program_id(0) == 0)
    def _():
        sums[...] = jnp.zeros_like(sums)

    wide[...] = w_ref[...].astype(jnp.float32)
    row_wide[0] = up_ref[...].astype(jnp.float32)
    row_wide[1] = down_ref[...].astype(jnp.float32)
    column_wide[0] = left_ref[...].astype(jnp.float32)
    column_wide[1] = right_ref[...].astype(jnp.float32)

    def read_bins(strip, lanes):
        row, column, side = strip
        return p_ref[row, column, side : side + 1, lanes]

    def read_joint(strip, lanes):
        row, column, side = strip
        own = wide[row, column, side : side + 1, lanes]
        if side < 2:
            return own * row_wide[side, column : column + 1, lanes]
        return own * column_wide[side - 2, row : row + 1, lanes]

    accumulate(dots, read_bins, read_joint, sums, p_ref.shape[-1])

    @pl.when(pl.program_id(0) == pl.num_programs(0) - 1)
    def _():
        finish(dots, sums, out_ref)


def strip_sums(kernel, strips, pixels, weights, halos, name):
    rows, columns, sides, length = pixels.shape
    width = chunk_width(length, WIDTH)
    dots = group(strips)
    block = (rows, columns, sides, width)
    halo_specs = [pl.BlockSpec((h.shape[0], width), lambda i: (0, i)) for h in halos]
    scratch = [pltpu.VMEM(block, jnp.float32)]
    if halos:
        scratch += [pltpu.VMEM((2, columns, width), jnp.float32), pltpu.VMEM((2, rows, width), jnp.float32)]
    scratch += [pltpu.VMEM((len(dots), 16 * SUBS * PER_DOT, 16 * SUBS * PER_DOT), jnp.float32)]
    return pl.pallas_call(
        functools.partial(kernel, dots),
        grid=(length // width,),
        in_specs=[pl.BlockSpec(block, lambda i: (0, 0, 0, i))] * 2 + halo_specs,
        out_specs=pl.BlockSpec((len(strips), 16, 16), lambda i: (0, 0, 0)),
        out_shape=jax.ShapeDtypeStruct((len(strips), 16, 16), jnp.float32),
        scratch_shapes=scratch,
        compiler_params=pltpu.CompilerParams(vmem_limit_bytes=56 * 1024 * 1024),
        cost_estimate=pl.CostEstimate(
            flops=len(strips) * length * 256 * 32,
            bytes_accessed=rows * columns * sides * length * 6,
            transcendentals=0,
        ),
        name=name,
    )(pixels, weights, *halos)


def shift(array, axis, step):
    count = lax.axis_size(axis)
    if step > 0:
        pairs = [(i, i + 1) for i in range(count - 1)]
    else:
        pairs = [(i + 1, i) for i in range(count - 1)]
    return lax.ppermute(array, axis, pairs)


def settle_kernel(
    inner, outer, shape, inner_ref, outer_ref, adjacency_ref, out_ref,
    row_in, column_in, own, other, tile, board, grid,
    near_send, near_recv, far_send, far_recv,
):
    rows, columns = shape
    x_count, y_count = lax.axis_size("gx"), lax.axis_size("gy")
    x_index, y_index = lax.axis_index("gx"), lax.axis_index("gy")
    devices = x_count * y_count
    me = x_index * y_count + y_index
    grid_rows, grid_columns = y_count * rows, x_count * columns
    lanes = grid.shape[1]

    def device(index):
        return {"gx": index // y_count, "gy": index % y_count}

    barrier = pltpu.get_barrier_semaphore()

    @pl.loop(1, devices)
    def _(step):
        pl.semaphore_signal(
            barrier, inc=1, device_id=device((me + step) % devices), device_id_type=pl.DeviceIdType.MESH
        )

    pl.semaphore_wait(barrier, devices - 1)

    up_copy = pltpu.make_async_remote_copy(
        src_ref=outer_ref.at[pl.ds(0, columns)], dst_ref=row_in,
        send_sem=near_send.at[0], recv_sem=near_recv.at[0],
        device_id={"gx": x_index, "gy": (y_index + y_count - 1) % y_count},
        device_id_type=pl.DeviceIdType.MESH,
    )
    left_copy = pltpu.make_async_remote_copy(
        src_ref=outer_ref.at[pl.ds(2 * columns, rows)], dst_ref=column_in,
        send_sem=near_send.at[1], recv_sem=near_recv.at[1],
        device_id={"gx": (x_index + x_count - 1) % x_count, "gy": y_index},
        device_id_type=pl.DeviceIdType.MESH,
    )
    up_copy.start()
    left_copy.start()

    where_inner = {strip: i for i, strip in enumerate(inner)}
    where_outer = {strip: i for i, strip in enumerate(outer)}

    def local(strip):
        if strip in where_inner:
            return inner_ref[where_inner[strip]]
        return outer_ref[where_outer[strip]]

    pairs = [(r, c, 1) for r in range(rows) for c in range(columns)]
    pairs += [(r, c, 3) for r in range(rows) for c in range(columns)]
    late = []
    for number, strip in enumerate(pairs):
        own[number] = local(strip)
        facing_strip = partner_of(strip)
        if facing_strip in where_inner:
            other[number] = local(facing_strip)
        else:
            late.append((number, strip))
    up_copy.wait()
    left_copy.wait()
    for number, (row, column, side) in late:
        other[number] = row_in[column] if side == 1 else column_in[row]

    count = len(pairs)
    centre = (
        16 * lax.broadcasted_iota(jnp.int32, (count, 16, 16), 1)
        + lax.broadcasted_iota(jnp.int32, (count, 16, 16), 2)
    ).astype(jnp.float32) + 0.5

    def over_bins(values):
        return jnp.sum(jnp.sum(values, axis=1, keepdims=True), axis=2, keepdims=True)

    def share_and_mean(values):
        total = over_bins(values)
        total = jnp.where(total > 0.0, total, 1.0)
        return values / total, over_bins(values * centre) / total

    own_share, own_mean = share_and_mean(own[...])
    other_share, other_mean = share_and_mean(other[...])
    gap = (own_share - other_share).reshape(count * 16, 16)
    low_a = lax.broadcasted_iota(jnp.int32, (16, 16), 0)
    low_b = lax.broadcasted_iota(jnp.int32, (16, 16), 1)
    high_a = lax.broadcasted_iota(jnp.int32, (count * 16, count * 16), 0)
    high_b = lax.broadcasted_iota(jnp.int32, (count * 16, count * 16), 1)
    within = (low_a <= low_b).astype(jnp.float32)
    before = ((high_a // 16 == high_b // 16) & (high_b < high_a)).astype(jnp.float32)
    exact = dict(precision=lax.Precision.HIGHEST, preferred_element_type=jnp.float32)
    running = jnp.dot(gap, within, **exact) + jnp.sum(
        jnp.dot(before, gap, **exact), axis=1, keepdims=True
    )
    distance = over_bins(jnp.abs(running).reshape(count, 16, 16))
    mismatch = (distance - jnp.abs(own_mean - other_mean)) / mismatch_scale
    confidence = (1.0 / (0.25 + mismatch * mismatch)).reshape(count, 1)
    offset = (jnp.log(other_mean) - jnp.log(own_mean)).reshape(count, 1)

    pair = lax.broadcasted_iota(jnp.int32, (count, lanes), 0)
    lane = lax.broadcasted_iota(jnp.int32, (count, lanes), 1)
    direction = pair // (rows * columns)
    pair_row = (pair % (rows * columns)) // columns
    spot = 2 * direction * grid_columns + x_index * columns + pair % columns
    placed = jnp.where(lane == spot, confidence, 0.0) + jnp.where(lane == spot + grid_columns, offset, 0.0)
    for row in range(rows):
        tile[row : row + 1] = jnp.sum(jnp.where(pair_row == row, placed, 0.0), axis=0, keepdims=True)
    board[x_index, y_index] = tile[...]

    def spread(index, source):
        return pltpu.make_async_remote_copy(
            src_ref=tile, dst_ref=board.at[source // y_count, source % y_count],
            send_sem=far_send.at[index], recv_sem=far_recv.at[source],
            device_id=device(index), device_id_type=pl.DeviceIdType.MESH,
        )

    @pl.loop(1, devices)
    def _(step):
        spread((me + step) % devices, me).start()

    @pl.loop(1, devices)
    def _(step):
        source = (me + step) % devices
        spread(source, source).wait_recv()

    for place in range(y_count):
        rows_here = board[0, place]
        for other_x in range(1, x_count):
            rows_here += board[other_x, place]
        grid[place * rows : (place + 1) * rows] = rows_here

    whole = grid[...]
    row_id = lax.broadcasted_iota(jnp.int32, (grid_rows, lanes), 0)
    lane_id = lax.broadcasted_iota(jnp.int32, (grid_rows, lanes), 1)

    def quantity(number, link, keep):
        values = whole if number == 0 else pltpu.roll(whole, lanes - number * grid_columns, 1)
        return jnp.where(keep, values, 0.0)

    def widened(index):
        flat = adjacency_ref[index]
        if lanes > grid_columns:
            blank = jnp.zeros((grid_rows, lanes - grid_columns), jnp.int32)
            flat = jnp.concatenate([flat, blank], axis=1)
        return flat

    keep_down = (widened(1) > 0) & (row_id < grid_rows - 1) & (lane_id < grid_columns)
    keep_right = (widened(0) > 0) & (lane_id < grid_columns - 1)
    down_conf = quantity(0, 1, keep_down)
    down_off = quantity(1, 1, keep_down)
    right_conf = quantity(2, 0, keep_right)
    right_off = quantity(3, 0, keep_right)
    up_conf, up_off = pltpu.roll(down_conf, 1, 0), -pltpu.roll(down_off, 1, 0)
    left_conf, left_off = pltpu.roll(right_conf, 1, 1), -pltpu.roll(right_off, 1, 1)
    confidence_sum = up_conf + down_conf + left_conf + right_conf
    denominator = anchor_weight + confidence_sum
    push = (
        up_conf * up_off + down_conf * down_off + left_conf * left_off + right_conf * right_off
    ) / denominator
    up_part, down_part = up_conf / denominator, down_conf / denominator
    left_part, right_part = left_conf / denominator, right_conf / denominator
    pull = confidence_sum / denominator
    tiles = grid_rows * grid_columns

    def mean_of(values):
        return jnp.sum(jnp.sum(values, axis=0, keepdims=True), axis=1, keepdims=True) / tiles

    def sweep(_, fresh):
        return (
            up_part * pltpu.roll(fresh, 1, 0)
            + down_part * pltpu.roll(fresh, grid_rows - 1, 0)
            + left_part * pltpu.roll(fresh, 1, 1)
            + right_part * pltpu.roll(fresh, lanes - 1, 1)
            + push
        ) - pull * mean_of(fresh)

    fresh = lax.fori_loop(0, ITERS - 1, sweep, push)
    log_gain = fresh - mean_of(fresh)
    result = jnp.zeros((rows, columns), jnp.float32)
    out_row = lax.broadcasted_iota(jnp.int32, (rows, columns), 0)
    out_column = lax.broadcasted_iota(jnp.int32, (rows, columns), 1)
    for row in range(rows):
        line = jnp.sum(jnp.where(row_id == y_index * rows + row, log_gain, 0.0), axis=0, keepdims=True)
        for column in range(columns):
            value = jnp.sum(
                jnp.where(lane_id[:1] == x_index * columns + column, line, 0.0), axis=1, keepdims=True
            )
            result += jnp.where((out_row == row) & (out_column == column), value, 0.0)
    out_ref[...] = result

    @pl.loop(1, devices)
    def _(step):
        spread((me + step) % devices, me).wait_send()


def settle(inner, outer, shape, inner_sums, outer_sums, adjacency):
    rows, columns = shape
    x_count, y_count = lax.axis_size("gx"), lax.axis_size("gy")
    devices = x_count * y_count
    lanes = -(-4 * x_count * columns // 128) * 128
    pairs = 2 * rows * columns
    vmem = pl.BlockSpec(memory_space=pltpu.VMEM)
    return pl.pallas_call(
        functools.partial(settle_kernel, inner, outer, shape),
        in_specs=[vmem] * 3,
        out_specs=vmem,
        out_shape=jax.ShapeDtypeStruct((rows, columns), jnp.float32),
        scratch_shapes=[
            pltpu.VMEM((columns, 16, 16), jnp.float32),
            pltpu.VMEM((rows, 16, 16), jnp.float32),
            pltpu.VMEM((pairs, 16, 16), jnp.float32),
            pltpu.VMEM((pairs, 16, 16), jnp.float32),
            pltpu.VMEM((rows, lanes), jnp.float32),
            pltpu.VMEM((x_count, y_count, rows, lanes), jnp.float32),
            pltpu.VMEM((y_count * rows, lanes), jnp.float32),
            pltpu.SemaphoreType.DMA((2,)),
            pltpu.SemaphoreType.DMA((2,)),
            pltpu.SemaphoreType.DMA((devices,)),
            pltpu.SemaphoreType.DMA((devices,)),
        ],
        compiler_params=pltpu.CompilerParams(collective_id=0, has_side_effects=True),
        name="settle",
    )(inner_sums, outer_sums, adjacency)


def body(pixels, weights, adjacency):
    rows, columns = pixels.shape[:2]
    up, down, left, right = edges(weights)
    from_up = shift(down, "gy", 1)
    from_down = shift(up, "gy", -1)
    from_left = shift(right, "gx", 1)
    from_right = shift(left, "gx", -1)
    inner = inner_strips(rows, columns)
    outer = outer_strips(rows, columns)
    inner_sums = strip_sums(inner_kernel, inner, pixels, weights, [], "inner")
    outer_sums = strip_sums(
        outer_kernel, outer, pixels, weights, [from_up, from_down, from_left, from_right], "outer"
    )
    return settle(inner, outer, (rows, columns), inner_sums, outer_sums, adjacency)


def solution(mesh):
    return jax.shard_map(
        body,
        mesh=mesh,
        in_specs=(P("gy", "gx", None, None), P("gy", "gx", None, None), P()),
        out_specs=P("gy", "gx"),
        check_vma=False,
    )
```

profile of v0, /device:TPU:0, one launch (start us, length us, event | category | flops | bytes accessed | tf_op | source)
XLA Modules:
  0.0 99.6 jit_solution(15253235956025314075)
XLA Ops:
  0.0 7.5 %edges.1 = (bf16[4,131072]{1,0:T(4,128)(2,1)}, bf16[4,131072]{1,0:T(4,128)(2,1)}, bf16[2,131072]{1,0:T(2,128)(2,1)}, bf16[2,131072]{1,0:T(2,128)(2,1)}) custom-call(bf16[2,4,4,131072]{3,2,1,0:T(4,128)(2,1)} %w_ref.5), custom_call_target="tpu_custom_call" | custom-call | tf_op jit(solution)/shard_map/edges/pallas_call | solution.py:117
  7.5 4.9 %collective-permute-start = (bf16[4,131072]{1,0:T(4,128)(2,1)}, bf16[4,131072]{1,0:T(4,128)(2,1)S(1)}, u32[]{:S(2)}, u32[]{:S(2)}) collective-permute-start(bf16[4,131072]{1,0:T(4,128)(2,1)} %get-tuple-element.9), channel_id=1, source_target_pairs={{0,1},{1,2},{2,3},{3,4},{4,5},{5,6},{6,7},{8,9},{9,10},{10,11},{11... | collective-permute-start | bytes 3145736 | tf_op jit(solution)/shard_map/ppermute | solution.py:217
  12.4 1.3 %collective-permute-start.1 = (bf16[4,131072]{1,0:T(4,128)(2,1)}, bf16[4,131072]{1,0:T(4,128)(2,1)S(1)}, u32[]{:S(2)}, u32[]{:S(2)}) collective-permute-start(bf16[4,131072]{1,0:T(4,128)(2,1)} %get-tuple-element.10), channel_id=1, source_target_pairs={{1,0},{2,1},{3,2},{4,3},{5,4},{6,5},{7,6},{9,8},{10,9},{11,10},{12... | collective-permute-start | bytes 3145736 | tf_op jit(solution)/shard_map/ppermute | solution.py:217
  13.7 1.5 %collective-permute-start.2 = (bf16[2,131072]{1,0:T(2,128)(2,1)}, bf16[2,131072]{1,0:T(2,128)(2,1)S(1)}, u32[]{:S(2)}, u32[]{:S(2)}) collective-permute-start(bf16[2,131072]{1,0:T(2,128)(2,1)} %get-tuple-element.11), channel_id=1, source_target_pairs={{0,8},{8,16},{16,24},{1,9},{9,17},{17,25},{2,10},{10,18},{18,26},{... | collective-permute-start | bytes 1572872 | tf_op jit(solution)/shard_map/ppermute | solution.py:217
  15.2 1.3 %collective-permute-start.3 = (bf16[2,131072]{1,0:T(2,128)(2,1)}, bf16[2,131072]{1,0:T(2,128)(2,1)S(1)}, u32[]{:S(2)}, u32[]{:S(2)}) collective-permute-start(bf16[2,131072]{1,0:T(2,128)(2,1)} %get-tuple-element.12), channel_id=1, source_target_pairs={{8,0},{16,8},{24,16},{9,1},{17,9},{25,17},{10,2},{18,10},{26,18},{... | collective-permute-start | bytes 1572872 | tf_op jit(solution)/shard_map/ppermute | solution.py:217
  16.5 26.5 %inner.1.inner_ref = f32[20,16,16]{2,1,0:T(8,128)} custom-call(s32[2,4,4,131072]{3,2,1,0:T(4,128)} %p_ref.3, bf16[2,4,4,131072]{3,2,1,0:T(4,128)(2,1)} %w_ref.5), custom_call_target="tpu_custom_call" | custom-call | flops 21474836480 | bytes 25165824 | tf_op jit(solution)/shard_map/inner/pallas_call | solution.py:194
  43.1 0.0 collective-permute-done.2.left_ref
  43.1 0.0 copy-start.2
  43.1 0.0 collective-permute-done.3.right_ref
  43.1 0.0 copy-start.3
  43.1 14.5 %collective-permute-done.up_ref = bf16[4,131072]{1,0:T(4,128)(2,1)S(1)} collective-permute-done((bf16[4,131072]{1,0:T(4,128)(2,1)}, bf16[4,131072]{1,0:T(4,128)(2,1)S(1)}, u32[]{:S(2)}, u32[]{:S(2)}) %collective-permute-start) | collective-permute-done | bytes 1048608 | tf_op jit(solution)/shard_map/ppermute | solution.py:217
  57.6 0.0 copy-start
  57.6 0.0 collective-permute-done.1.down_ref
  57.6 0.0 copy-done.2
  57.6 0.0 copy-done.3
  57.6 1.0 %copy-done = bf16[4,131072]{1,0:T(4,128)(2,1)} copy-done((bf16[4,131072]{1,0:T(4,128)(2,1)}, bf16[4,131072]{1,0:T(4,128)(2,1)S(1)}, u32[]{:S(2)}) %copy-start) | copy-done | bytes 1048600
  58.6 0.0 copy-start.1
  58.6 1.0 copy-done.1
  59.6 19.1 %outer.1.outer_ref = f32[12,16,16]{2,1,0:T(8,128)} custom-call(s32[2,4,4,131072]{3,2,1,0:T(4,128)} %p_ref.3, bf16[2,4,4,131072]{3,2,1,0:T(4,128)(2,1)} %w_ref.5, bf16[4,131072]{1,0:T(4,128)(2,1)} %copy-done, bf16[4,131072]{1,0:T(4,128)(2,1)} %copy-done.1, bf16[2,131072]{1,0:T(2,128)(2,1)} %copy-done.2, bf16[2,131072]{1,0:T(2,128)(2,1)} %copy-done.3), custom_call_target="tpu_custom_call" | custom-call | flops 12884901888 | bytes 25165824 | tf_op jit(solution)/shard_map/outer/pallas_call | solution.py:194
  78.7 19.6 %settle.1 = f32[2,4]{1,0:T(2,128)} custom-call(f32[20,16,16]{2,1,0:T(8,128)} %inner.1.inner_ref, f32[12,16,16]{2,1,0:T(8,128)} %outer.1.outer_ref, s32[2,16,16]{2,1,0:T(8,128)} %adjacency_ref.1), custom_call_target="tpu_custom_call" | custom-call | tf_op jit(solution)/shard_map/settle/pallas_call | solution.py:419
  98.3 1.2 %copy.5 = f32[2,4]{1,0:T(2,128)} copy(f32[2,4]{1,0:T(2,128)} %settle.1) | data formatting | bytes 64
Async XLA Ops:
  7.5 50.1 %collective-permute-start = (bf16[4,131072]{1,0:T(4,128)(2,1)}, bf16[4,131072]{1,0:T(4,128)(2,1)S(1)}, u32[]{:S(2)}, u32[]{:S(2)}) collective-permute-start(bf16[4,131072]{1,0:T(4,128)(2,1)} %get-tuple-element.9), channel_id=1, source_target_pairs={{0,1},{1,2},{2,3},{3,4},{4,5},{5,6},{6,7},{8,9},{9,10},{10,11},{11... | collective-permute-start | bytes 3145736 | tf_op jit(solution)/shard_map/ppermute | solution.py:217
  12.4 45.1 %collective-permute-start.1 = (bf16[4,131072]{1,0:T(4,128)(2,1)}, bf16[4,131072]{1,0:T(4,128)(2,1)S(1)}, u32[]{:S(2)}, u32[]{:S(2)}) collective-permute-start(bf16[4,131072]{1,0:T(4,128)(2,1)} %get-tuple-element.10), channel_id=1, source_target_pairs={{1,0},{2,1},{3,2},{4,3},{5,4},{6,5},{7,6},{9,8},{10,9},{11,10},{12... | collective-permute-start | bytes 3145736 | tf_op jit(solution)/shard_map/ppermute | solution.py:217
  13.7 29.3 %collective-permute-start.2 = (bf16[2,131072]{1,0:T(2,128)(2,1)}, bf16[2,131072]{1,0:T(2,128)(2,1)S(1)}, u32[]{:S(2)}, u32[]{:S(2)}) collective-permute-start(bf16[2,131072]{1,0:T(2,128)(2,1)} %get-tuple-element.11), channel_id=1, source_target_pairs={{0,8},{8,16},{16,24},{1,9},{9,17},{17,25},{2,10},{10,18},{18,26},{... | collective-permute-start | bytes 1572872 | tf_op jit(solution)/shard_map/ppermute | solution.py:217
  15.2 27.8 %collective-permute-start.3 = (bf16[2,131072]{1,0:T(2,128)(2,1)}, bf16[2,131072]{1,0:T(2,128)(2,1)S(1)}, u32[]{:S(2)}, u32[]{:S(2)}) collective-permute-start(bf16[2,131072]{1,0:T(2,128)(2,1)} %get-tuple-element.12), channel_id=1, source_target_pairs={{8,0},{16,8},{24,16},{9,1},{17,9},{25,17},{10,2},{18,10},{26,18},{... | collective-permute-start | bytes 1572872 | tf_op jit(solution)/shard_map/ppermute | solution.py:217
  43.1 14.5 %copy-start.2 = (bf16[2,131072]{1,0:T(2,128)(2,1)}, bf16[2,131072]{1,0:T(2,128)(2,1)S(1)}, u32[]{:S(2)}) copy-start(bf16[2,131072]{1,0:T(2,128)(2,1)S(1)} %collective-permute-done.2.left_ref) | copy-start | bytes 1572868
  43.1 14.5 %copy-start.3 = (bf16[2,131072]{1,0:T(2,128)(2,1)}, bf16[2,131072]{1,0:T(2,128)(2,1)S(1)}, u32[]{:S(2)}) copy-start(bf16[2,131072]{1,0:T(2,128)(2,1)S(1)} %collective-permute-done.3.right_ref) | copy-start | bytes 1572868
  57.6 1.0 %copy-start = (bf16[4,131072]{1,0:T(4,128)(2,1)}, bf16[4,131072]{1,0:T(4,128)(2,1)S(1)}, u32[]{:S(2)}) copy-start(bf16[4,131072]{1,0:T(4,128)(2,1)S(1)} %collective-permute-done.up_ref) | copy-start | bytes 3145732
  58.6 1.0 copy-start.1
where the time goes:
time: 99.9 us; the launch traced here: 99.6 us
  Pallas kernels  72.8 us (73%)
  waiting for transfers between devices  14.5 us (15%)
  starting transfers between devices  9 us (9%)
  local copies, waits for them, and re-layouts  3.22 us (3%)
    pallas_call x2, Pallas kernels, strip_sums(): pl.pallas_call(functools.partial(kernel, dots), grid=(length // width,),...  45.7 us
    pallas_call x1, Pallas kernels, settle(): pl.pallas_call(functools.partial(settle_kernel, inner, outer, shape), in_...  19.6 us
    ppermute x4, waiting for transfers between devices, shift(): return lax.ppermute(array, axis, pairs)  14.5 us
    ppermute x4, starting transfers between devices, shift(): return lax.ppermute(array, axis, pairs)  9 us
    pallas_call x1, Pallas kernels, edges(): pl.pallas_call(edges_kernel, grid=(length // width,), in_specs=[pl.BlockS...  7.51 us
    unnamed x9, local copies, waits for them, and re-layouts  3.22 us
  transfers between devices with their start and end apart: 4, of which 1 were waited for; matrix products, arithmetic and copies ran while one was open for 0% of the time, Pallas kernels for 27%

commit v1 on v0

v1 whole, which is shorter than its diff:
```python
import functools
import jax
import jax.numpy as jnp
from jax import lax
from jax.experimental import pallas as pl
from jax.experimental.pallas import tpu as pltpu
from jax.sharding import PartitionSpec as P

ITERS = 20
CHUNKS = 16
LEVELS = 16

anchor_weight = 0.5
mismatch_scale = 8.0


def partner_of(strip):
    row, column, side = strip
    return [
        (row - 1, column, 1),
        (row + 1, column, 0),
        (row, column - 1, 3),
        (row, column + 1, 2),
    ][side]


def border(direction, rows, columns):
    return [
        [(0, column, 0) for column in range(columns)],
        [(rows - 1, column, 1) for column in range(columns)],
        [(row, 0, 2) for row in range(rows)],
        [(row, columns - 1, 3) for row in range(rows)],
    ][direction]


def fold_of(count):
    return max(1, 4 // count)


def roll_rows(values, shift):
    shift = shift % 8
    return values if shift == 0 else pltpu.roll(values, shift, 1)


def wide(values):
    return values.astype(jnp.float32).reshape(values.shape[0] // 8, 8, 128)


def chunk_count(steps):
    count = CHUNKS
    while steps % (count * 16):
        count //= 2
    return count


def strips_kernel(
    shape, chunks, p_ref, w_ref, out_ref,
    p_all, w_all, up_out, down_out, left_out, right_out, up_in, down_in, left_in, right_in, joint, sums,
    p_sem, w_sem, send_sem, recv_sem,
):
    rows, columns, steps = shape
    tiles = [(r, c) for r in range(rows) for c in range(columns)]
    span = steps // chunks
    height = span * 4
    outs = [up_out, down_out, left_out, right_out]
    ins = [up_in, down_in, left_in, right_in]
    x_count, y_count = lax.axis_size("gx"), lax.axis_size("gy")
    x_index, y_index = lax.axis_index("gx"), lax.axis_index("gy")
    present = [y_index > 0, y_index < y_count - 1, x_index > 0, x_index < x_count - 1]
    target = [
        {"gx": x_index, "gy": y_index - 1},
        {"gx": x_index, "gy": y_index + 1},
        {"gx": x_index - 1, "gy": y_index},
        {"gx": x_index + 1, "gy": y_index},
    ]
    borders = [border(d, rows, columns) for d in range(4)]
    folds = [fold_of(len(b)) for b in borders]
    parts = max(folds)

    def chunk(index, size):
        return pl.ds(pl.multiple_of(index * size, 16), size)

    def fetch(index, source, target_ref, sem):
        window = chunk(index, height)
        return pltpu.make_async_copy(
            source.at[:, :, window, :], target_ref.at[:, :, window, :], sem.at[index]
        )

    def send(direction, index):
        window = chunk(index, span * len(borders[direction]))
        opposite = direction ^ 1
        return pltpu.make_async_remote_copy(
            src_ref=outs[direction].at[window, :],
            dst_ref=ins[opposite].at[window, :],
            send_sem=send_sem.at[direction, index],
            recv_sem=recv_sem.at[opposite, index],
            device_id=target[direction],
            device_id_type=pl.DeviceIdType.MESH,
        )

    @pl.loop(0, chunks)
    def _(index):
        fetch(index, w_ref, w_all, w_sem).start()

    @pl.loop(0, chunks)
    def _(index):
        fetch(index, p_ref, p_all, p_sem).start()

    barrier = pltpu.get_barrier_semaphore()
    for direction in range(4):
        @pl.when(present[direction])
        def _():
            pl.semaphore_signal(
                barrier, inc=1, device_id=target[direction], device_id_type=pl.DeviceIdType.MESH
            )

    neighbours = sum(jnp.where(here, 1, 0) for here in present)
    pl.semaphore_wait(barrier, neighbours)

    side = lax.broadcasted_iota(jnp.int32, (1, 8, 128), 1) % 4

    @pl.loop(0, chunks)
    def _(index):
        fetch(index, w_ref, w_all, w_sem).wait()
        for direction in range(4):
            strips, fold = borders[direction], folds[direction]
            for first in range(0, len(strips), 4):
                group = strips[first : first + 4]
                length = height // fold

                @pl.loop(0, length // 16)
                def _(step):
                    total = None
                    for part in range(fold):
                        start = pl.multiple_of(index * height + part * length + step * 16, 16)
                        for number, (row, column, own) in enumerate(group):
                            place = part * len(group) + number
                            value = roll_rows(wide(w_all[row, column, pl.ds(start, 16), :]), place - own)
                            total = value if total is None else jnp.where(side == place, value, total)
                    start = pl.multiple_of(
                        index * span * len(strips) + (first // 4) * height + step * 16, 16
                    )
                    outs[direction][pl.ds(start, 16), :] = total.reshape(16, 128).astype(jnp.bfloat16)

        for direction in range(4):
            @pl.when(present[direction])
            def _():
                send(direction, index).start()

    for direction in range(4):
        @pl.when(jnp.logical_not(present[direction]))
        def _():
            ins[direction][...] = jnp.zeros_like(ins[direction])

    sums[...] = jnp.zeros_like(sums)

    @pl.loop(0, chunks)
    def _(index):
        fetch(index, p_ref, p_all, p_sem).wait()
        for direction in range(4):
            @pl.when(present[direction])
            def _():
                send(direction ^ 1, index).wait_recv()

        length = height // parts
        for part in range(parts):
            @pl.loop(0, length // 16)
            def _(step):
                local = part * length + step * 16
                start = pl.multiple_of(index * height + local, 16)
                values = {tile: wide(w_all[tile[0], tile[1], pl.ds(start, 16), :]) for tile in tiles}

                def facing(tile, own):
                    row, column, other = partner_of((tile[0], tile[1], own))
                    if (row, column) in values:
                        return values[row, column]
                    count, fold = len(borders[own]), folds[own]
                    number = tile[1] if own < 2 else tile[0]
                    piece = part * fold // parts
                    place = piece * count + number if fold > 1 else number % 4
                    offset = pl.multiple_of(
                        index * span * count + (number // 4) * height * (fold == 1)
                        + local - piece * (height // fold), 16
                    )
                    return roll_rows(wide(ins[own][pl.ds(offset, 16), :]), other - place)

                for tile in tiles:
                    from_after = jnp.where(side == 0, facing(tile, 1), facing(tile, 3))
                    from_before = jnp.where(side == 1, facing(tile, 0), facing(tile, 2))
                    partner = jnp.where(side % 2 == 0, roll_rows(from_before, -1), roll_rows(from_after, 1))
                    product = (values[tile] * partner).reshape(16, 128).astype(jnp.bfloat16)
                    joint[tile[0], tile[1], pl.ds(pl.multiple_of(local, 16), 16), :] = product

        for number, (row, column) in enumerate(tiles):
            bins = p_all[row, column, chunk(index, height), :].astype(jnp.int16)
            both = joint[row, column]
            pieces = range(height // 16)
            bins = jnp.concatenate([bins[16 * i : 16 * i + 16] for i in pieces], axis=1)
            both = jnp.concatenate([both[16 * i : 16 * i + 16] for i in pieces], axis=1)
            upper, lower = bins & 240, bins & 15
            zero, one = jnp.zeros_like(both), jnp.ones_like(both)
            left = jnp.concatenate([jnp.where(upper == 16 * i, both, zero) for i in range(LEVELS)], axis=0)
            right = jnp.concatenate([jnp.where(lower == i, one, zero) for i in range(LEVELS)], axis=0)
            sums[number] += lax.dot_general(
                left, right, (((1,), (1,)), ((), ())), preferred_element_type=jnp.float32
            )

    a = lax.broadcasted_iota(jnp.int32, (256, 256), 0)
    b = lax.broadcasted_iota(jnp.int32, (256, 256), 1)
    diagonal = a % 16 == b % 16
    packed = []
    for number in range(len(tiles)):
        kept = jnp.where(diagonal, sums[number], 0.0)
        packed.append(jnp.sum(kept.reshape(16, 16, 256), axis=1))
    packed = jnp.concatenate(packed, axis=0)
    lane = lax.broadcasted_iota(jnp.int32, (256, 64), 0)
    spot = lax.broadcasted_iota(jnp.int32, (256, 64), 1)
    pick = ((lane // 16 == spot % 16) & (lane % 4 == spot // 16)).astype(jnp.float32)
    result = jnp.dot(packed, pick, precision=lax.Precision.HIGHEST, preferred_element_type=jnp.float32)
    for number in range(len(tiles)):
        for own in range(4):
            out_ref[number * 4 + own] = result[number * 16 : number * 16 + 16, own * 16 : own * 16 + 16]

    @pl.loop(0, chunks)
    def _(index):
        for direction in range(4):
            @pl.when(present[direction])
            def _():
                send(direction, index).wait_send()


def strip_sums(pixels, weights):
    rows, columns, sides, length = pixels.shape
    steps = length // 128
    chunks = chunk_count(steps)

    def stacked(array):
        array = array.reshape(rows, columns, sides, steps, 128)
        return array.transpose(0, 1, 3, 2, 4).reshape(rows, columns, steps * sides, 128)

    def halo(count):
        return pltpu.VMEM((steps * count, 128), jnp.bfloat16)

    halos = [halo(columns), halo(columns), halo(rows), halo(rows)]
    return pl.pallas_call(
        functools.partial(strips_kernel, (rows, columns, steps), chunks),
        in_specs=[pl.BlockSpec(memory_space=pl.ANY)] * 2,
        out_specs=pl.BlockSpec(memory_space=pltpu.VMEM),
        out_shape=jax.ShapeDtypeStruct((rows * columns * sides, 16, 16), jnp.float32),
        scratch_shapes=[
            pltpu.VMEM((rows, columns, steps * sides, 128), jnp.int32),
            pltpu.VMEM((rows, columns, steps * sides, 128), jnp.bfloat16),
            *halos,
            *halos,
            pltpu.VMEM((rows, columns, steps * sides // chunks, 128), jnp.bfloat16),
            pltpu.VMEM((rows * columns, 256, 256), jnp.float32),
            pltpu.SemaphoreType.DMA((chunks,)),
            pltpu.SemaphoreType.DMA((chunks,)),
            pltpu.SemaphoreType.DMA((4, chunks)),
            pltpu.SemaphoreType.DMA((4, chunks)),
        ],
        compiler_params=pltpu.CompilerParams(
            collective_id=1, has_side_effects=True, vmem_limit_bytes=60 * 1024 * 1024
        ),
        name="strips",
    )(stacked(pixels), stacked(weights))


def settle_kernel(
    shape, hist_ref, adjacency_ref, out_ref,
    up_row, left_column,
    row_in, column_in, own, other, tile, board, grid,
    near_send, near_recv, far_send, far_recv,
):
    rows, columns = shape
    x_count, y_count = lax.axis_size("gx"), lax.axis_size("gy")
    x_index, y_index = lax.axis_index("gx"), lax.axis_index("gy")
    devices = x_count * y_count
    me = x_index * y_count + y_index
    grid_rows, grid_columns = y_count * rows, x_count * columns
    lanes = grid.shape[1]

    def device(index):
        return {"gx": index // y_count, "gy": index % y_count}

    for column in range(columns):
        up_row[column] = hist_ref[column * 4]
    for row in range(rows):
        left_column[row] = hist_ref[row * columns * 4 + 2]

    barrier = pltpu.get_barrier_semaphore()

    @pl.loop(1, devices)
    def _(step):
        pl.semaphore_signal(
            barrier, inc=1, device_id=device((me + step) % devices), device_id_type=pl.DeviceIdType.MESH
        )

    pl.semaphore_wait(barrier, devices - 1)

    up_copy = pltpu.make_async_remote_copy(
        src_ref=up_row, dst_ref=row_in,
        send_sem=near_send.at[0], recv_sem=near_recv.at[0],
        device_id={"gx": x_index, "gy": (y_index + y_count - 1) % y_count},
        device_id_type=pl.DeviceIdType.MESH,
    )
    left_copy = pltpu.make_async_remote_copy(
        src_ref=left_column, dst_ref=column_in,
        send_sem=near_send.at[1], recv_sem=near_recv.at[1],
        device_id={"gx": (x_index + x_count - 1) % x_count, "gy": y_index},
        device_id_type=pl.DeviceIdType.MESH,
    )
    up_copy.start()
    left_copy.start()

    def local(strip):
        row, column, side = strip
        return hist_ref[(row * columns + column) * 4 + side]

    pairs = [(r, c, 1) for r in range(rows) for c in range(columns)]
    pairs += [(r, c, 3) for r in range(rows) for c in range(columns)]
    late = []
    for number, strip in enumerate(pairs):
        own[number] = local(strip)
        facing_strip = partner_of(strip)
        if facing_strip[0] < rows and facing_strip[1] < columns:
            other[number] = local(facing_strip)
        else:
            late.append((number, strip))
    up_copy.wait()
    left_copy.wait()
    for number, (row, column, side) in late:
        other[number] = row_in[column] if side == 1 else column_in[row]

    count = len(pairs)
    centre = (
        16 * lax.broadcasted_iota(jnp.int32, (count, 16, 16), 1)
        + lax.broadcasted_iota(jnp.int32, (count, 16, 16), 2)
    ).astype(jnp.float32) + 0.5

    def over_bins(values):
        return jnp.sum(jnp.sum(values, axis=1, keepdims=True), axis=2, keepdims=True)

    def share_and_mean(values):
        total = over_bins(values)
        total = jnp.where(total > 0.0, total, 1.0)
        return values / total, over_bins(values * centre) / total

    own_share, own_mean = share_and_mean(own[...])
    other_share, other_mean = share_and_mean(other[...])
    gap = (own_share - other_share).reshape(count * 16, 16)
    low_a = lax.broadcasted_iota(jnp.int32, (16, 16), 0)
    low_b = lax.broadcasted_iota(jnp.int32, (16, 16), 1)
    high_a = lax.broadcasted_iota(jnp.int32, (count * 16, count * 16), 0)
    high_b = lax.broadcasted_iota(jnp.int32, (count * 16, count * 16), 1)
    within = (low_a <= low_b).astype(jnp.float32)
    before = ((high_a // 16 == high_b // 16) & (high_b < high_a)).astype(jnp.float32)
    exact = dict(precision=lax.Precision.HIGHEST, preferred_element_type=jnp.float32)
    running = jnp.dot(gap, within, **exact) + jnp.sum(
        jnp.dot(before, gap, **exact), axis=1, keepdims=True
    )
    distance = over_bins(jnp.abs(running).reshape(count, 16, 16))
    mismatch = (distance - jnp.abs(own_mean - other_mean)) / mismatch_scale
    confidence = (1.0 / (0.25 + mismatch * mismatch)).reshape(count, 1)
    offset = (jnp.log(other_mean) - jnp.log(own_mean)).reshape(count, 1)

    pair = lax.broadcasted_iota(jnp.int32, (count, lanes), 0)
    lane = lax.broadcasted_iota(jnp.int32, (count, lanes), 1)
    direction = pair // (rows * columns)
    pair_row = (pair % (rows * columns)) // columns
    spot = 2 * direction * grid_columns + x_index * columns + pair % columns
    placed = jnp.where(lane == spot, confidence, 0.0) + jnp.where(lane == spot + grid_columns, offset, 0.0)
    for row in range(rows):
        tile[row : row + 1] = jnp.sum(jnp.where(pair_row == row, placed, 0.0), axis=0, keepdims=True)
    board[x_index, y_index] = tile[...]

    def spread(index, source):
        return pltpu.make_async_remote_copy(
            src_ref=tile, dst_ref=board.at[source // y_count, source % y_count],
            send_sem=far_send.at[index], recv_sem=far_recv.at[source],
            device_id=device(index), device_id_type=pl.DeviceIdType.MESH,
        )

    @pl.loop(1, devices)
    def _(step):
        spread((me + step) % devices, me).start()

    @pl.loop(1, devices)
    def _(step):
        source = (me + step) % devices
        spread(source, source).wait_recv()

    for place in range(y_count):
        rows_here = board[0, place]
        for other_x in range(1, x_count):
            rows_here += board[other_x, place]
        grid[place * rows : (place + 1) * rows] = rows_here

    whole = grid[...]
    row_id = lax.broadcasted_iota(jnp.int32, (grid_rows, lanes), 0)
    lane_id = lax.broadcasted_iota(jnp.int32, (grid_rows, lanes), 1)

    def quantity(number, link, keep):
        values = whole if number == 0 else pltpu.roll(whole, lanes - number * grid_columns, 1)
        return jnp.where(keep, values, 0.0)

    def widened(index):
        flat = adjacency_ref[index]
        if lanes > grid_columns:
            blank = jnp.zeros((grid_rows, lanes - grid_columns), jnp.int32)
            flat = jnp.concatenate([flat, blank], axis=1)
        return flat

    keep_down = (widened(1) > 0) & (row_id < grid_rows - 1) & (lane_id < grid_columns)
    keep_right = (widened(0) > 0) & (lane_id < grid_columns - 1)
    down_conf = quantity(0, 1, keep_down)
    down_off = quantity(1, 1, keep_down)
    right_conf = quantity(2, 0, keep_right)
    right_off = quantity(3, 0, keep_right)
    up_conf, up_off = pltpu.roll(down_conf, 1, 0), -pltpu.roll(down_off, 1, 0)
    left_conf, left_off = pltpu.roll(right_conf, 1, 1), -pltpu.roll(right_off, 1, 1)
    confidence_sum = up_conf + down_conf + left_conf + right_conf
    denominator = anchor_weight + confidence_sum
    push = (
        up_conf * up_off + down_conf * down_off + left_conf * left_off + right_conf * right_off
    ) / denominator
    up_part, down_part = up_conf / denominator, down_conf / denominator
    left_part, right_part = left_conf / denominator, right_conf / denominator
    pull = confidence_sum / denominator
    tiles = grid_rows * grid_columns

    def mean_of(values):
        return jnp.sum(jnp.sum(values, axis=0, keepdims=True), axis=1, keepdims=True) / tiles

    def sweep(_, fresh):
        return (
            up_part * pltpu.roll(fresh, 1, 0)
            + down_part * pltpu.roll(fresh, grid_rows - 1, 0)
            + left_part * pltpu.roll(fresh, 1, 1)
            + right_part * pltpu.roll(fresh, lanes - 1, 1)
            + push
        ) - pull * mean_of(fresh)

    fresh = lax.fori_loop(0, ITERS - 1, sweep, push)
    log_gain = fresh - mean_of(fresh)
    result = jnp.zeros((rows, columns), jnp.float32)
    out_row = lax.broadcasted_iota(jnp.int32, (rows, columns), 0)
    out_column = lax.broadcasted_iota(jnp.int32, (rows, columns), 1)
    for row in range(rows):
        line = jnp.sum(jnp.where(row_id == y_index * rows + row, log_gain, 0.0), axis=0, keepdims=True)
        for column in range(columns):
            value = jnp.sum(
                jnp.where(lane_id[:1] == x_index * columns + column, line, 0.0), axis=1, keepdims=True
            )
            result += jnp.where((out_row == row) & (out_column == column), value, 0.0)
    out_ref[...] = result

    @pl.loop(1, devices)
    def _(step):
        spread((me + step) % devices, me).wait_send()


def settle(shape, sums, adjacency):
    rows, columns = shape
    x_count, y_count = lax.axis_size("gx"), lax.axis_size("gy")
    devices = x_count * y_count
    lanes = -(-4 * x_count * columns // 128) * 128
    pairs = 2 * rows * columns
    vmem = pl.BlockSpec(memory_space=pltpu.VMEM)
    return pl.pallas_call(
        functools.partial(settle_kernel, shape),
        in_specs=[vmem] * 2,
        out_specs=vmem,
        out_shape=jax.ShapeDtypeStruct((rows, columns), jnp.float32),
        scratch_shapes=[
            pltpu.VMEM((columns, 16, 16), jnp.float32),
            pltpu.VMEM((rows, 16, 16), jnp.float32),
            pltpu.VMEM((columns, 16, 16), jnp.float32),
            pltpu.VMEM((rows, 16, 16), jnp.float32),
            pltpu.VMEM((pairs, 16, 16), jnp.float32),
            pltpu.VMEM((pairs, 16, 16), jnp.float32),
            pltpu.VMEM((rows, lanes), jnp.float32),
            pltpu.VMEM((x_count, y_count, rows, lanes), jnp.float32),
            pltpu.VMEM((y_count * rows, lanes), jnp.float32),
            pltpu.SemaphoreType.DMA((2,)),
            pltpu.SemaphoreType.DMA((2,)),
            pltpu.SemaphoreType.DMA((devices,)),
            pltpu.SemaphoreType.DMA((devices,)),
        ],
        compiler_params=pltpu.CompilerParams(collective_id=0, has_side_effects=True),
        name="settle",
    )(sums, adjacency)


def body(pixels, weights, adjacency):
    rows, columns = pixels.shape[:2]
    return settle((rows, columns), strip_sums(pixels, weights), adjacency)


def solution(mesh):
    return jax.shard_map(
        body,
        mesh=mesh,
        in_specs=(P("gy", "gx", None, None), P("gy", "gx", None, None), P()),
        out_specs=P("gy", "gx"),
        check_vma=False,
    )
```

time: 99.9 us -> 97.6 us (0.977)
  Pallas kernels: 72.8 us -> 96.1 us
  waiting for transfers between devices: 14.5 us -> 0 us
  starting transfers between devices: 9 us -> 0 us
  local copies, waits for them, and re-layouts: 3.22 us -> 1.23 us
    pallas_call x4 -> x2, Pallas kernels: 72.8 us -> 96.1 us  [the longest x1 59.1 us: strip_sums(): pl.pallas_call(functools.partial(strips_kernel, (rows, columns, steps), c...]
    ppermute x4 -> x0, waiting for transfers between devices: 14.5 us -> none  [shift(): return lax.ppermute(array, axis, pairs)]
    ppermute x4 -> x0, starting transfers between devices: 9 us -> none  [shift(): return lax.ppermute(array, axis, pairs)]
    unnamed x9 -> x1, local copies, waits for them, and re-layouts: 3.22 us -> 1.23 us
  transfers between devices with their start and end apart: 4 -> 0, of which waited for: 1 -> 0; matrix products, arithmetic and copies ran while one was open for 0% -> 0% of each run, Pallas kernels for 27% -> 0%
where the time goes in v1:
time: 97.6 us; the launch traced here: 97.4 us
  Pallas kernels  96.1 us (98%)
  local copies, waits for them, and re-layouts  1.23 us (1%)
    pallas_call x1, Pallas kernels, strip_sums(): pl.pallas_call(functools.partial(strips_kernel, (rows, columns, steps), c...  59.1 us
    pallas_call x1, Pallas kernels, settle(): pl.pallas_call(functools.partial(settle_kernel, shape), in_specs=[vmem] *...  37.1 us

profile of v1, /device:TPU:0, one launch (start us, length us, event | category | flops | bytes accessed | tf_op | source)
XLA Modules:
  0.0 97.4 jit_solution(2425766353350377741)
XLA Ops:
  0.0 59.1 %strips.1.hist_ref = f32[32,16,16]{2,1,0:T(8,128)} custom-call(s32[2,4,4096,128]{3,2,1,0:T(8,128)} %bitcast.10, bf16[2,4,4096,128]{3,2,1,0:T(8,128)(2,1)} %bitcast.11), custom_call_target="tpu_custom_call" | custom-call | tf_op jit(solution)/shard_map/strips/pallas_call | solution.py:245
  59.1 37.1 %settle.1 = f32[2,4]{1,0:T(2,128)} custom-call(f32[32,16,16]{2,1,0:T(8,128)} %strips.1.hist_ref, s32[2,16,16]{2,1,0:T(8,128)} %adjacency_ref.1), custom_call_target="tpu_custom_call" | custom-call | tf_op jit(solution)/shard_map/settle/pallas_call | solution.py:470
  96.2 1.2 %copy.7 = f32[2,4]{1,0:T(2,128)} copy(f32[2,4]{1,0:T(2,128)} %settle.1) | data formatting | bytes 64

commit v2 on v1

--- a/solution.py
+++ b/solution.py
@@ -7,7 +7,7 @@
 from jax.sharding import PartitionSpec as P
 
 ITERS = 20
-CHUNKS = 16
+CHUNKS = 8
 LEVELS = 16
 
 anchor_weight = 0.5
@@ -33,8 +33,30 @@
     ][direction]
 
 
-def fold_of(count):
-    return max(1, 4 // count)
+def groups_of(strips):
+    groups, first = [], 0
+    while first < len(strips):
+        size = min(4, len(strips) - first)
+        size = 2 if size == 3 else size
+        groups.append(strips[first : first + size])
+        first += size
+    return groups
+
+
+def inner_groups(rows, columns):
+    down = [(row, column, 1) for row in range(rows - 1) for column in range(columns)]
+    right = [(row, column, 3) for row in range(rows) for column in range(columns - 1)]
+    groups = []
+    for strips in groups_of(down) + groups_of(right):
+        groups += [strips, [partner_of(strip) for strip in strips]]
+    return groups
+
+
+def all_groups(rows, columns):
+    groups = inner_groups(rows, columns)
+    for direction in range(4):
+        groups += groups_of(border(direction, rows, columns))
+    return groups
 
 
 def roll_rows(values, shift):
@@ -42,8 +64,34 @@
     return values if shift == 0 else pltpu.roll(values, shift, 1)
 
 
-def wide(values):
-    return values.astype(jnp.float32).reshape(values.shape[0] // 8, 8, 128)
+def gather(read, strips, start, height, side):
+    length = height * len(strips) // 4
+    total = None
+    for place in range(4):
+        row, column, own = strips[place % len(strips)]
+        value = read[row, column, pl.ds(start + place // len(strips) * length, length), :]
+        if value.dtype == jnp.bfloat16:
+            value = value.astype(jnp.float32)
+        value = roll_rows(value.reshape(length // 8, 8, 128), place - own)
+        total = value if total is None else jnp.where(side == place, value, total)
+    return total
+
+
+def flat(values, dtype):
+    return values.reshape(values.shape[0] * 8, 128).astype(dtype)
+
+
+def across(values):
+    return jnp.concatenate([values[i : i + 16] for i in range(0, values.shape[0], 16)], axis=1)
+
+
+def outer_product(bins, joint):
+    bins, joint = across(bins), across(joint)
+    upper, lower = bins & 240, bins & 15
+    zero, one = jnp.zeros_like(joint), jnp.ones_like(joint)
+    left = jnp.concatenate([jnp.where(upper == 16 * i, joint, zero) for i in range(LEVELS)], axis=0)
+    right = jnp.concatenate([jnp.where(lower == i, one, zero) for i in range(LEVELS)], axis=0)
+    return lax.dot_general(left, right, (((1,), (1,)), ((), ())), preferred_element_type=jnp.float32)
 
 
 def chunk_count(steps):
@@ -55,11 +103,10 @@
 
 def strips_kernel(
     shape, chunks, p_ref, w_ref, out_ref,
-    p_all, w_all, up_out, down_out, left_out, right_out, up_in, down_in, left_in, right_in, joint, sums,
+    p_all, w_all, up_out, down_out, left_out, right_out, up_in, down_in, left_in, right_in, sums,
     p_sem, w_sem, send_sem, recv_sem,
 ):
     rows, columns, steps = shape
-    tiles = [(r, c) for r in range(rows) for c in range(columns)]
     span = steps // chunks
     height = span * 4
     outs = [up_out, down_out, left_out, right_out]
@@ -74,8 +121,9 @@
         {"gx": x_index + 1, "gy": y_index},
     ]
     borders = [border(d, rows, columns) for d in range(4)]
-    folds = [fold_of(len(b)) for b in borders]
-    parts = max(folds)
+    inner = inner_groups(rows, columns)
+    groups = all_groups(rows, columns)
+    side = lax.broadcasted_iota(jnp.int32, (1, 8, 128), 1) % 4
 
     def chunk(index, size):
         return pl.ds(pl.multiple_of(index * size, 16), size)
@@ -98,13 +146,14 @@
             device_id_type=pl.DeviceIdType.MESH,
         )
 
+    def await_halo(direction, index):
+        @pl.when(present[direction])
+        def _():
+            send(direction ^ 1, index).wait_recv()
+
     @pl.loop(0, chunks)
     def _(index):
         fetch(index, w_ref, w_all, w_sem).start()
-
-    @pl.loop(0, chunks)
-    def _(index):
-        fetch(index, p_ref, p_all, p_sem).start()
 
     barrier = pltpu.get_barrier_semaphore()
     for direction in range(4):
@@ -114,33 +163,23 @@
                 barrier, inc=1, device_id=target[direction], device_id_type=pl.DeviceIdType.MESH
             )
 
+    @pl.loop(0, chunks)
+    def _(index):
+        fetch(index, p_ref, p_all, p_sem).start()
+
     neighbours = sum(jnp.where(here, 1, 0) for here in present)
     pl.semaphore_wait(barrier, neighbours)
-
-    side = lax.broadcasted_iota(jnp.int32, (1, 8, 128), 1) % 4
 
     @pl.loop(0, chunks)
     def _(index):
         fetch(index, w_ref, w_all, w_sem).wait()
         for direction in range(4):
-            strips, fold = borders[direction], folds[direction]
-            for first in range(0, len(strips), 4):
-                group = strips[first : first + 4]
-                length = height // fold
-
-                @pl.loop(0, length // 16)
-                def _(step):
-                    total = None
-                    for part in range(fold):
-                        start = pl.multiple_of(index * height + part * length + step * 16, 16)
-                        for number, (row, column, own) in enumerate(group):
-                            place = part * len(group) + number
-                            value = roll_rows(wide(w_all[row, column, pl.ds(start, 16), :]), place - own)
-                            total = value if total is None else jnp.where(side == place, value, total)
-                    start = pl.multiple_of(
-                        index * span * len(strips) + (first // 4) * height + step * 16, 16
-                    )
-                    outs[direction][pl.ds(start, 16), :] = total.reshape(16, 128).astype(jnp.bfloat16)
+            base = index * span * len(borders[direction])
+            for strips in groups_of(borders[direction]):
+                length = height * len(strips) // 4
+                total = gather(w_all, strips, pl.multiple_of(index * height, 16), height, side)
+                outs[direction][pl.ds(pl.multiple_of(base, 16), length), :] = flat(total, jnp.bfloat16)
+                base += length
 
         for direction in range(4):
             @pl.when(present[direction])
@@ -154,62 +193,46 @@
 
     sums[...] = jnp.zeros_like(sums)
 
+    def bins_of(strips, index):
+        return flat(gather(p_all, strips, pl.multiple_of(index * height, 16), height, side), jnp.int16)
+
+    def edge(direction, index):
+        base = index * span * len(borders[direction])
+        for strips in groups_of(borders[direction]):
+            length = height * len(strips) // 4
+            window = pl.ds(pl.multiple_of(base, 16), length)
+            mine = outs[direction][window, :].astype(jnp.float32)
+            joint = (mine * ins[direction][window, :].astype(jnp.float32)).astype(jnp.bfloat16)
+            sums[groups.index(strips)] += outer_product(bins_of(strips, index), joint)
+            base += length
+
     @pl.loop(0, chunks)
     def _(index):
         fetch(index, p_ref, p_all, p_sem).wait()
-        for direction in range(4):
-            @pl.when(present[direction])
-            def _():
-                send(direction ^ 1, index).wait_recv()
-
-        length = height // parts
-        for part in range(parts):
-            @pl.loop(0, length // 16)
-            def _(step):
-                local = part * length + step * 16
-                start = pl.multiple_of(index * height + local, 16)
-                values = {tile: wide(w_all[tile[0], tile[1], pl.ds(start, 16), :]) for tile in tiles}
-
-                def facing(tile, own):
-                    row, column, other = partner_of((tile[0], tile[1], own))
-                    if (row, column) in values:
-                        return values[row, column]
-                    count, fold = len(borders[own]), folds[own]
-                    number = tile[1] if own < 2 else tile[0]
-                    piece = part * fold // parts
-                    place = piece * count + number if fold > 1 else number % 4
-                    offset = pl.multiple_of(
-                        index * span * count + (number // 4) * height * (fold == 1)
-                        + local - piece * (height // fold), 16
-                    )
-                    return roll_rows(wide(ins[own][pl.ds(offset, 16), :]), other - place)
-
-                for tile in tiles:
-                    from_after = jnp.where(side == 0, facing(tile, 1), facing(tile, 3))
-                    from_before = jnp.where(side == 1, facing(tile, 0), facing(tile, 2))
-                    partner = jnp.where(side % 2 == 0, roll_rows(from_before, -1), roll_rows(from_after, 1))
-                    product = (values[tile] * partner).reshape(16, 128).astype(jnp.bfloat16)
-                    joint[tile[0], tile[1], pl.ds(pl.multiple_of(local, 16), 16), :] = product
-
-        for number, (row, column) in enumerate(tiles):
-            bins = p_all[row, column, chunk(index, height), :].astype(jnp.int16)
-            both = joint[row, column]
-            pieces = range(height // 16)
-            bins = jnp.concatenate([bins[16 * i : 16 * i + 16] for i in pieces], axis=1)
-            both = jnp.concatenate([both[16 * i : 16 * i + 16] for i in pieces], axis=1)
-            upper, lower = bins & 240, bins & 15
-            zero, one = jnp.zeros_like(both), jnp.ones_like(both)
-            left = jnp.concatenate([jnp.where(upper == 16 * i, both, zero) for i in range(LEVELS)], axis=0)
-            right = jnp.concatenate([jnp.where(lower == i, one, zero) for i in range(LEVELS)], axis=0)
-            sums[number] += lax.dot_general(
-                left, right, (((1,), (1,)), ((), ())), preferred_element_type=jnp.float32
-            )
+        await_halo(2, index)
+        await_halo(3, index)
+        for number in range(0, len(inner), 2):
+            start = pl.multiple_of(index * height, 16)
+            first = gather(w_all, inner[number], start, height, side)
+            second = gather(w_all, inner[number + 1], start, height, side)
+            joint = flat(first * second, jnp.bfloat16)
+            sums[number] += outer_product(bins_of(inner[number], index), joint)
+            sums[number + 1] += outer_product(bins_of(inner[number + 1], index), joint)
+        edge(2, index)
+        edge(3, index)
+
+    @pl.loop(0, chunks)
+    def _(index):
+        await_halo(0, index)
+        await_halo(1, index)
+        edge(0, index)
+        edge(1, index)
 
     a = lax.broadcasted_iota(jnp.int32, (256, 256), 0)
     b = lax.broadcasted_iota(jnp.int32, (256, 256), 1)
     diagonal = a % 16 == b % 16
     packed = []
-    for number in range(len(tiles)):
+    for number in range(len(groups)):
         kept = jnp.where(diagonal, sums[number], 0.0)
         packed.append(jnp.sum(kept.reshape(16, 16, 256), axis=1))
     packed = jnp.concatenate(packed, axis=0)
@@ -217,9 +240,13 @@
     spot = lax.broadcasted_iota(jnp.int32, (256, 64), 1)
     pick = ((lane // 16 == spot % 16) & (lane % 4 == spot // 16)).astype(jnp.float32)
     result = jnp.dot(packed, pick, precision=lax.Precision.HIGHEST, preferred_element_type=jnp.float32)
-    for number in range(len(tiles)):
-        for own in range(4):
-            out_ref[number * 4 + own] = result[number * 16 : number * 16 + 16, own * 16 : own * 16 + 16]
+    for number, strips in enumerate(groups):
+        for first, (row, column, own) in enumerate(strips):
+            parts = [
+                result[number * 16 : number * 16 + 16, place * 16 : place * 16 + 16]
+                for place in range(first, 4, len(strips))
+            ]
+            out_ref[(row * columns + column) * 4 + own] = sum(parts[1:], parts[0])
 
     @pl.loop(0, chunks)
     def _(index):
@@ -252,8 +279,7 @@
             pltpu.VMEM((rows, columns, steps * sides, 128), jnp.bfloat16),
             *halos,
             *halos,
-            pltpu.VMEM((rows, columns, steps * sides // chunks, 128), jnp.bfloat16),
-            pltpu.VMEM((rows * columns, 256, 256), jnp.float32),
+            pltpu.VMEM((len(all_groups(rows, columns)), 256, 256), jnp.float32),
             pltpu.SemaphoreType.DMA((chunks,)),
             pltpu.SemaphoreType.DMA((chunks,)),
             pltpu.SemaphoreType.DMA((4, chunks)),

time: 97.6 us -> 74.1 us (0.76)
  Pallas kernels: 96.1 us -> 72.7 us
    pallas_call x1, Pallas kernels: 37.1 us -> 22.5 us  [settle(): pl.pallas_call(functools.partial(settle_kernel, shape), in_specs=[vmem] *...]
    pallas_call x1, Pallas kernels: 59.1 us -> 50.2 us  [strip_sums(): pl.pallas_call(functools.partial(strips_kernel, (rows, columns, steps), c...]
where the time goes in v2:
time: 74.1 us; the launch traced here: 73.9 us
  Pallas kernels  72.7 us (98%)
  local copies, waits for them, and re-layouts  1.23 us (2%)
    pallas_call x1, Pallas kernels, strip_sums(): pl.pallas_call(functools.partial(strips_kernel, (rows, columns, steps), c...  50.2 us
    pallas_call x1, Pallas kernels, settle(): pl.pallas_call(functools.partial(settle_kernel, shape), in_specs=[vmem] *...  22.5 us

profile of v2, /device:TPU:0, one launch (start us, length us, event | category | flops | bytes accessed | tf_op | source)
XLA Modules:
  0.0 73.9 jit_solution(7965646956460817793)
XLA Ops:
  0.0 50.2 %strips.1.hist_ref = f32[32,16,16]{2,1,0:T(8,128)} custom-call(s32[2,4,4096,128]{3,2,1,0:T(8,128)} %bitcast.10, bf16[2,4,4096,128]{3,2,1,0:T(8,128)(2,1)} %bitcast.11), custom_call_target="tpu_custom_call" | custom-call | tf_op jit(solution)/shard_map/strips/pallas_call | solution.py:272
  50.2 22.5 %settle.1 = f32[2,4]{1,0:T(2,128)} custom-call(f32[32,16,16]{2,1,0:T(8,128)} %strips.1.hist_ref, s32[2,16,16]{2,1,0:T(8,128)} %adjacency_ref.1), custom_call_target="tpu_custom_call" | custom-call | tf_op jit(solution)/shard_map/settle/pallas_call | solution.py:496
  72.7 1.2 %copy.7 = f32[2,4]{1,0:T(2,128)} copy(f32[2,4]{1,0:T(2,128)} %settle.1) | data formatting | bytes 64

commit v3 on v2

v3 whole, which is shorter than its diff:
```python
import functools
import jax
import jax.numpy as jnp
from jax import lax
from jax.experimental import pallas as pl
from jax.experimental.pallas import tpu as pltpu
from jax.sharding import PartitionSpec as P

ITERS = 20
CHUNKS = 8
LEVELS = 16

anchor_weight = 0.5
mismatch_scale = 8.0


def partner_of(strip):
    row, column, side = strip
    return [
        (row - 1, column, 1),
        (row + 1, column, 0),
        (row, column - 1, 3),
        (row, column + 1, 2),
    ][side]


def border(direction, rows, columns):
    return [
        [(0, column, 0) for column in range(columns)],
        [(rows - 1, column, 1) for column in range(columns)],
        [(row, 0, 2) for row in range(rows)],
        [(row, columns - 1, 3) for row in range(rows)],
    ][direction]


def groups_of(strips):
    groups, first = [], 0
    while first < len(strips):
        size = min(4, len(strips) - first)
        size = 2 if size == 3 else size
        groups.append(strips[first : first + size])
        first += size
    return groups


def inner_groups(rows, columns):
    down = [(row, column, 1) for row in range(rows - 1) for column in range(columns)]
    right = [(row, column, 3) for row in range(rows) for column in range(columns - 1)]
    groups = []
    for strips in groups_of(down) + groups_of(right):
        groups += [strips, [partner_of(strip) for strip in strips]]
    return groups


def all_groups(rows, columns):
    groups = inner_groups(rows, columns)
    for direction in range(4):
        groups += groups_of(border(direction, rows, columns))
    return groups


def roll_rows(values, shift):
    shift = shift % 8
    return values if shift == 0 else pltpu.roll(values, shift, 1)


def gather(read, strips, start, height, side):
    length = height * len(strips) // 4
    total = None
    for place in range(4):
        row, column, own = strips[place % len(strips)]
        value = read[row, column, pl.ds(start + place // len(strips) * length, length), :]
        if value.dtype == jnp.bfloat16:
            value = value.astype(jnp.float32)
        value = roll_rows(value.reshape(length // 8, 8, 128), place - own)
        total = value if total is None else jnp.where(side == place, value, total)
    return total


def flat(values, dtype):
    return values.reshape(values.shape[0] * 8, 128).astype(dtype)


def across(values):
    return jnp.concatenate([values[i : i + 16] for i in range(0, values.shape[0], 16)], axis=1)


def outer_product(bins, joint):
    bins, joint = across(bins), across(joint)
    upper, lower = bins & 240, bins & 15
    zero, one = jnp.zeros_like(joint), jnp.ones_like(joint)
    left = jnp.concatenate([jnp.where(upper == 16 * i, joint, zero) for i in range(LEVELS)], axis=0)
    right = jnp.concatenate([jnp.where(lower == i, one, zero) for i in range(LEVELS)], axis=0)
    return lax.dot_general(left, right, (((1,), (1,)), ((), ())), preferred_element_type=jnp.float32)


def chunk_count(steps):
    count = CHUNKS
    while steps % (count * 16):
        count //= 2
    return count


def kernel(
    shape, chunks, p_ref, w_ref, adjacency_hbm, out_ref,
    p_all, w_all, up_out, down_out, left_out, right_out, up_in, down_in, left_in, right_in, sums,
    hist, row_out, column_out, row_in, column_in, tile, board, grid, adjacency_ref,
    p_sem, w_sem, send_sem, recv_sem, near_send, near_recv, far_send, far_recv, adjacency_sem,
):
    rows, columns, steps = shape
    span = steps // chunks
    height = span * 4
    outs = [up_out, down_out, left_out, right_out]
    ins = [up_in, down_in, left_in, right_in]
    x_count, y_count = lax.axis_size("gx"), lax.axis_size("gy")
    x_index, y_index = lax.axis_index("gx"), lax.axis_index("gy")
    devices = x_count * y_count
    me = x_index * y_count + y_index
    present = [y_index > 0, y_index < y_count - 1, x_index > 0, x_index < x_count - 1]
    target = [
        {"gx": x_index, "gy": y_index - 1},
        {"gx": x_index, "gy": y_index + 1},
        {"gx": x_index - 1, "gy": y_index},
        {"gx": x_index + 1, "gy": y_index},
    ]
    borders = [border(d, rows, columns) for d in range(4)]
    inner = inner_groups(rows, columns)
    groups = all_groups(rows, columns)
    side = lax.broadcasted_iota(jnp.int32, (1, 8, 128), 1) % 4

    def chunk(index, size):
        return pl.ds(pl.multiple_of(index * size, 16), size)

    def fetch(index, source, target_ref, sem):
        window = chunk(index, height)
        return pltpu.make_async_copy(
            source.at[:, :, window, :], target_ref.at[:, :, window, :], sem.at[index]
        )

    def send(direction, index):
        window = chunk(index, span * len(borders[direction]))
        opposite = direction ^ 1
        return pltpu.make_async_remote_copy(
            src_ref=outs[direction].at[window, :],
            dst_ref=ins[opposite].at[window, :],
            send_sem=send_sem.at[direction],
            recv_sem=recv_sem.at[opposite, index],
            device_id=target[direction],
            device_id_type=pl.DeviceIdType.MESH,
        )

    def await_halo(direction, index):
        @pl.when(present[direction])
        def _():
            send(direction ^ 1, index).wait_recv()

    @pl.loop(0, chunks)
    def _(index):
        fetch(index, w_ref, w_all, w_sem).start()

    barrier = pltpu.get_barrier_semaphore()

    def device(index):
        return {"gx": index // y_count, "gy": index % y_count}

    @pl.loop(1, devices)
    def _(step):
        pl.semaphore_signal(
            barrier, inc=1, device_id=device((me + step) % devices), device_id_type=pl.DeviceIdType.MESH
        )

    def pack(index):
        fetch(index, w_ref, w_all, w_sem).wait()
        for direction in range(4):
            base = index * span * len(borders[direction])
            for strips in groups_of(borders[direction]):
                length = height * len(strips) // 4
                total = gather(w_all, strips, pl.multiple_of(index * height, 16), height, side)
                outs[direction][pl.ds(pl.multiple_of(base, 16), length), :] = flat(total, jnp.bfloat16)
                base += length

    def send_all(index):
        for direction in range(4):
            @pl.when(present[direction])
            def _():
                send(direction, index).start()

    @pl.loop(0, chunks)
    def _(index):
        fetch(index, p_ref, p_all, p_sem).start()

    adjacency_copy = pltpu.make_async_copy(adjacency_hbm, adjacency_ref, adjacency_sem)
    adjacency_copy.start()
    pack(0)
    pl.semaphore_wait(barrier, devices - 1)

    @pl.loop(1, chunks)
    def _(index):
        pack(index)
        send_all(index - 1)

    send_all(chunks - 1)

    for direction in range(4):
        @pl.when(jnp.logical_not(present[direction]))
        def _():
            ins[direction][...] = jnp.zeros_like(ins[direction])

    sums[...] = jnp.zeros_like(sums)

    def bins_of(strips, index):
        return flat(gather(p_all, strips, pl.multiple_of(index * height, 16), height, side), jnp.int16)

    def edge(direction, index):
        base = index * span * len(borders[direction])
        for strips in groups_of(borders[direction]):
            length = height * len(strips) // 4
            window = pl.ds(pl.multiple_of(base, 16), length)
            mine = outs[direction][window, :].astype(jnp.float32)
            joint = (mine * ins[direction][window, :].astype(jnp.float32)).astype(jnp.bfloat16)
            sums[groups.index(strips)] += outer_product(bins_of(strips, index), joint)
            base += length

    @pl.loop(0, chunks)
    def _(index):
        fetch(index, p_ref, p_all, p_sem).wait()
        await_halo(2, index)
        await_halo(3, index)
        for number in range(0, len(inner), 2):
            start = pl.multiple_of(index * height, 16)
            first = gather(w_all, inner[number], start, height, side)
            second = gather(w_all, inner[number + 1], start, height, side)
            joint = flat(first * second, jnp.bfloat16)
            sums[number] += outer_product(bins_of(inner[number], index), joint)
            sums[number + 1] += outer_product(bins_of(inner[number + 1], index), joint)
        edge(2, index)
        edge(3, index)

    near = [
        (row_out, row_in, near_send.at[0], near_recv.at[0], target[0]),
        (column_out, column_in, near_send.at[1], near_recv.at[1], target[2]),
    ]

    def near_copy(number):
        source, destination, send_side, recv_side, where = near[number]
        return pltpu.make_async_remote_copy(
            src_ref=source, dst_ref=destination, send_sem=send_side, recv_sem=recv_side,
            device_id=where, device_id_type=pl.DeviceIdType.MESH,
        )

    def finish(numbers):
        a = lax.broadcasted_iota(jnp.int32, (256, 256), 0)
        b = lax.broadcasted_iota(jnp.int32, (256, 256), 1)
        packed = []
        for number in numbers:
            kept = jnp.where(a % 16 == b % 16, sums[number], 0.0)
            packed.append(jnp.sum(kept.reshape(16, 16, 256), axis=1))
        packed = jnp.concatenate(packed, axis=0)
        lane = lax.broadcasted_iota(jnp.int32, (256, 64), 0)
        spot = lax.broadcasted_iota(jnp.int32, (256, 64), 1)
        pick = ((lane // 16 == spot % 16) & (lane % 4 == spot // 16)).astype(jnp.float32)
        result = jnp.dot(packed, pick, precision=lax.Precision.HIGHEST, preferred_element_type=jnp.float32)
        for order, number in enumerate(numbers):
            strips = groups[number]
            for first, strip in enumerate(strips):
                parts = [
                    result[order * 16 : order * 16 + 16, place * 16 : place * 16 + 16]
                    for place in range(first, 4, len(strips))
                ]
                hist[place_of(strip)] = sum(parts[1:], parts[0])

    def place_of(strip):
        row, column, own = strip
        return (row * columns + column) * 4 + own

    lanes = grid.shape[1]

    def terms(pairs):
        count = len(pairs)
        own = jnp.stack([hist[place_of(strip)] for strip in pairs])
        other = []
        for strip in pairs:
            row, column, _ = partner_of(strip)
            if row == rows:
                other.append(row_in[column])
            elif column == columns:
                other.append(column_in[row])
            else:
                other.append(hist[place_of(partner_of(strip))])
        other = jnp.stack(other)
        centre = (
            16 * lax.broadcasted_iota(jnp.int32, (count, 16, 16), 1)
            + lax.broadcasted_iota(jnp.int32, (count, 16, 16), 2)
        ).astype(jnp.float32) + 0.5

        def over_bins(values):
            return jnp.sum(jnp.sum(values, axis=1, keepdims=True), axis=2, keepdims=True)

        def share_and_mean(values):
            total = over_bins(values)
            total = jnp.where(total > 0.0, total, 1.0)
            return values / total, over_bins(values * centre) / total

        own_share, own_mean = share_and_mean(own)
        other_share, other_mean = share_and_mean(other)
        gap = (own_share - other_share).reshape(count * 16, 16)
        low_a = lax.broadcasted_iota(jnp.int32, (16, 16), 0)
        low_b = lax.broadcasted_iota(jnp.int32, (16, 16), 1)
        high_a = lax.broadcasted_iota(jnp.int32, (count * 16, count * 16), 0)
        high_b = lax.broadcasted_iota(jnp.int32, (count * 16, count * 16), 1)
        within = (low_a <= low_b).astype(jnp.float32)
        before = ((high_a // 16 == high_b // 16) & (high_b < high_a)).astype(jnp.float32)
        exact = dict(precision=lax.Precision.HIGHEST, preferred_element_type=jnp.float32)
        running = jnp.dot(gap, within, **exact) + jnp.sum(
            jnp.dot(before, gap, **exact), axis=1, keepdims=True
        )
        distance = over_bins(jnp.abs(running).reshape(count, 16, 16))
        mismatch = (distance - jnp.abs(own_mean - other_mean)) / mismatch_scale
        confidence = (1.0 / (0.25 + mismatch * mismatch)).reshape(count, 1)
        offset = (jnp.log(other_mean) - jnp.log(own_mean)).reshape(count, 1)
        lane = lax.broadcasted_iota(jnp.int32, (1, lanes), 1)
        lines = [jnp.zeros((1, lanes), jnp.float32) for _ in range(rows)]
        for number, (row, column, own_side) in enumerate(pairs):
            spot = (own_side - 1) * grid_columns + x_index * columns + column
            lines[row] = jnp.where(lane == spot, confidence[number : number + 1], lines[row])
            lines[row] = jnp.where(
                lane == spot + grid_columns, offset[number : number + 1], lines[row]
            )
        return lines

    grid_rows, grid_columns = y_count * rows, x_count * columns
    number_of = {strip: n for n, strips in enumerate(groups) for strip in strips}
    late = sorted({number_of[strip] for strip in borders[0] + borders[1]})
    finish([n for n in range(len(groups)) if n not in late])
    for row in range(rows):
        column_out[row] = hist[place_of((row, 0, 2))]

    @pl.when(present[2])
    def _():
        near_copy(1).start()

    @pl.loop(0, chunks)
    def _(index):
        await_halo(0, index)
        await_halo(1, index)
        edge(0, index)
        edge(1, index)

    finish(late)
    for column in range(columns):
        row_out[column] = hist[place_of((0, column, 0))]

    @pl.when(present[0])
    def _():
        near_copy(0).start()

    @pl.when(present[3])
    def _():
        near_copy(1).wait_recv()

    @pl.when(jnp.logical_not(present[3]))
    def _():
        column_in[...] = jnp.zeros_like(column_in)

    early = [(r, c, 1) for r in range(rows - 1) for c in range(columns)]
    early += [(r, c, 3) for r in range(rows) for c in range(columns)]
    lines = terms(early)

    @pl.when(present[1])
    def _():
        near_copy(0).wait_recv()

    @pl.when(jnp.logical_not(present[1]))
    def _():
        row_in[...] = jnp.zeros_like(row_in)

    more = terms(borders[1])
    for row in range(rows):
        tile[row : row + 1] = lines[row] + more[row]
    board[me] = tile[...]

    def spread(index, source):
        return pltpu.make_async_remote_copy(
            src_ref=tile, dst_ref=board.at[source],
            send_sem=far_send, recv_sem=far_recv,
            device_id=device(index), device_id_type=pl.DeviceIdType.MESH,
        )

    @pl.loop(1, devices)
    def _(step):
        spread((me + step) % devices, me).start()

    for number in range(2):
        @pl.when(present[2 * number])
        def _():
            near_copy(number).wait_send()

    for direction in range(4):
        @pl.when(present[direction])
        def _():
            pltpu.make_async_remote_copy(
                src_ref=outs[direction], dst_ref=ins[direction ^ 1],
                send_sem=send_sem.at[direction], recv_sem=recv_sem.at[direction, 0],
                device_id=target[direction], device_id_type=pl.DeviceIdType.MESH,
            ).wait_send()

    others = pltpu.make_async_remote_copy(
        src_ref=board.at[pl.ds(1, devices - 1)], dst_ref=board.at[pl.ds(1, devices - 1)],
        send_sem=far_send, recv_sem=far_recv,
        device_id=device((me + 1) % devices), device_id_type=pl.DeviceIdType.MESH,
    )
    others.wait_send()
    others.wait_recv()

    for place in range(y_count):
        rows_here = board[place]
        for other_x in range(1, x_count):
            rows_here += board[other_x * y_count + place]
        grid[place * rows : (place + 1) * rows] = rows_here

    adjacency_copy.wait()
    whole = grid[...]
    row_id = lax.broadcasted_iota(jnp.int32, (grid_rows, lanes), 0)
    lane_id = lax.broadcasted_iota(jnp.int32, (grid_rows, lanes), 1)

    def quantity(number, link, keep):
        values = whole if number == 0 else pltpu.roll(whole, lanes - number * grid_columns, 1)
        return jnp.where(keep, values, 0.0)

    def widened(index):
        flat = adjacency_ref[index]
        if lanes > grid_columns:
            blank = jnp.zeros((grid_rows, lanes - grid_columns), jnp.int32)
            flat = jnp.concatenate([flat, blank], axis=1)
        return flat

    keep_down = (widened(1) > 0) & (row_id < grid_rows - 1) & (lane_id < grid_columns)
    keep_right = (widened(0) > 0) & (lane_id < grid_columns - 1)
    down_conf = quantity(0, 1, keep_down)
    down_off = quantity(1, 1, keep_down)
    right_conf = quantity(2, 0, keep_right)
    right_off = quantity(3, 0, keep_right)
    up_conf, up_off = pltpu.roll(down_conf, 1, 0), -pltpu.roll(down_off, 1, 0)
    left_conf, left_off = pltpu.roll(right_conf, 1, 1), -pltpu.roll(right_off, 1, 1)
    confidence_sum = up_conf + down_conf + left_conf + right_conf
    denominator = anchor_weight + confidence_sum
    push = (
        up_conf * up_off + down_conf * down_off + left_conf * left_off + right_conf * right_off
    ) / denominator
    up_part, down_part = up_conf / denominator, down_conf / denominator
    left_part, right_part = left_conf / denominator, right_conf / denominator
    pull = confidence_sum / denominator
    tiles = grid_rows * grid_columns

    def mean_of(values):
        return jnp.sum(jnp.sum(values, axis=0, keepdims=True), axis=1, keepdims=True) / tiles

    def sweep(_, fresh):
        return (
            up_part * pltpu.roll(fresh, 1, 0)
            + down_part * pltpu.roll(fresh, grid_rows - 1, 0)
            + left_part * pltpu.roll(fresh, 1, 1)
            + right_part * pltpu.roll(fresh, lanes - 1, 1)
            + push
        ) - pull * mean_of(fresh)

    fresh = lax.fori_loop(0, ITERS - 1, sweep, push)
    log_gain = fresh - mean_of(fresh)
    result = jnp.zeros((rows, columns), jnp.float32)
    out_row = lax.broadcasted_iota(jnp.int32, (rows, columns), 0)
    out_column = lax.broadcasted_iota(jnp.int32, (rows, columns), 1)
    for row in range(rows):
        line = jnp.sum(jnp.where(row_id == y_index * rows + row, log_gain, 0.0), axis=0, keepdims=True)
        for column in range(columns):
            value = jnp.sum(
                jnp.where(lane_id[:1] == x_index * columns + column, line, 0.0), axis=1, keepdims=True
            )
            result += jnp.where((out_row == row) & (out_column == column), value, 0.0)
    out_ref[...] = result


def body(pixels, weights, adjacency):
    rows, columns, sides, length = pixels.shape
    steps = length // 128
    chunks = chunk_count(steps)
    x_count, y_count = lax.axis_size("gx"), lax.axis_size("gy")
    devices = x_count * y_count
    lanes = -(-4 * x_count * columns // 128) * 128

    def stacked(array):
        array = array.reshape(rows, columns, sides, steps, 128)
        return array.transpose(0, 1, 3, 2, 4).reshape(rows, columns, steps * sides, 128)

    def halo(count):
        return pltpu.VMEM((steps * count, 128), jnp.bfloat16)

    halos = [halo(columns), halo(columns), halo(rows), halo(rows)]
    return pl.pallas_call(
        functools.partial(kernel, (rows, columns, steps), chunks),
        in_specs=[pl.BlockSpec(memory_space=pl.ANY)] * 3,
        out_specs=pl.BlockSpec(memory_space=pltpu.VMEM),
        out_shape=pltpu.VMEM((rows, columns), jnp.float32),
        scratch_shapes=[
            pltpu.VMEM((rows, columns, steps * sides, 128), jnp.int32),
            pltpu.VMEM((rows, columns, steps * sides, 128), jnp.bfloat16),
            *halos,
            *halos,
            pltpu.VMEM((len(all_groups(rows, columns)), 256, 256), jnp.float32),
            pltpu.VMEM((rows * columns * sides, 16, 16), jnp.float32),
            *([pltpu.VMEM((columns, 16, 16), jnp.float32), pltpu.VMEM((rows, 16, 16), jnp.float32)] * 2),
            pltpu.VMEM((rows, lanes), jnp.float32),
            pltpu.VMEM((devices, rows, lanes), jnp.float32),
            pltpu.VMEM((y_count * rows, lanes), jnp.float32),
            pltpu.VMEM(adjacency.shape, jnp.int32),
            pltpu.SemaphoreType.DMA((chunks,)),
            pltpu.SemaphoreType.DMA((chunks,)),
            pltpu.SemaphoreType.DMA((4,)),
            pltpu.SemaphoreType.DMA((4, chunks)),
            pltpu.SemaphoreType.DMA((2,)),
            pltpu.SemaphoreType.DMA((2,)),
            pltpu.SemaphoreType.DMA,
            pltpu.SemaphoreType.DMA,
            pltpu.SemaphoreType.DMA,
        ],
        compiler_params=pltpu.CompilerParams(
            collective_id=0, has_side_effects=True, vmem_limit_bytes=60 * 1024 * 1024
        ),
        name="equalise",
    )(stacked(pixels), stacked(weights), adjacency)


def solution(mesh):
    return jax.shard_map(
        body,
        mesh=mesh,
        in_specs=(P("gy", "gx", None, None), P("gy", "gx", None, None), P()),
        out_specs=P("gy", "gx"),
        check_vma=False,
    )
```

time: 74.1 us -> 66.4 us (0.90)
  Pallas kernels: 72.7 us -> 65.6 us
    pallas_call x2 -> x1, Pallas kernels: 72.7 us -> 65.6 us  [body(): pl.pallas_call(functools.partial(kernel, (rows, columns, steps), chunks),...]
where the time goes in v3:
time: 66.4 us; the launch traced here: 66.2 us
  Pallas kernels  65.6 us (99%)
    pallas_call x1, Pallas kernels, body(): pl.pallas_call(functools.partial(kernel, (rows, columns, steps), chunks),...  65.6 us

profile of v3, /device:TPU:0, one launch (start us, length us, event | category | flops | bytes accessed | tf_op | source)
XLA Modules:
  0.0 66.2 jit_solution(2272909694404739553)
XLA Ops:
  0.0 65.6 %equalise.1 = f32[2,4]{1,0:T(2,128)S(1)} custom-call(s32[2,4,4096,128]{3,2,1,0:T(8,128)} %bitcast.10, bf16[2,4,4096,128]{3,2,1,0:T(8,128)(2,1)} %bitcast.11, s32[2,16,16]{2,1,0:T(8,128)} %adjacency_hbm.1), custom_call_target="tpu_custom_call" | custom-call | tf_op jit(solution)/shard_map/equalise/pallas_call | solution.py:498
  65.7 0.6 copy.7

commit v4 on v3

--- a/solution.py
+++ b/solution.py
@@ -106,6 +106,7 @@
     p_all, w_all, up_out, down_out, left_out, right_out, up_in, down_in, left_in, right_in, sums,
     hist, row_out, column_out, row_in, column_in, tile, board, grid, adjacency_ref,
     p_sem, w_sem, send_sem, recv_sem, near_send, near_recv, far_send, far_recv, adjacency_sem,
+    relay_in, relay_send, relay_recv,
 ):
     rows, columns, steps = shape
     span = steps // chunks
@@ -179,11 +180,78 @@
                 outs[direction][pl.ds(pl.multiple_of(base, 16), length), :] = flat(total, jnp.bfloat16)
                 base += length
 
-    def send_all(index):
-        for direction in range(4):
+    relays = x_count == 4 and y_count % 2 == 0
+    layers = y_count // 2
+    layer, parity = y_index // 2, y_index % 2
+    up_count, down_count = chunks * layer // layers, chunks * (layers - 1 - layer) // layers
+    out_count = jnp.where(parity == 1, down_count, up_count)
+    relay_count = jnp.where(parity == 1, up_count, down_count)
+    relay_chunk = span * columns
+
+    def to_relay(far, index):
+        return pltpu.make_async_remote_copy(
+            src_ref=outs[far].at[chunk(index, relay_chunk), :],
+            dst_ref=relay_in.at[chunk(index, relay_chunk), :],
+            send_sem=send_sem.at[far],
+            recv_sem=relay_recv.at[index],
+            device_id=target[1 - far],
+            device_id_type=pl.DeviceIdType.MESH,
+        )
+
+    def forward(far, index):
+        step = -2 if far == 1 else 2
+        return pltpu.make_async_remote_copy(
+            src_ref=relay_in.at[chunk(index, relay_chunk), :],
+            dst_ref=ins[far].at[chunk(index, relay_chunk), :],
+            send_sem=relay_send.at[index],
+            recv_sem=recv_sem.at[far, index],
+            device_id={"gx": x_index, "gy": y_index + step},
+            device_id_type=pl.DeviceIdType.MESH,
+        )
+
+    def pass_on(index):
+        piece = index - (chunks - relay_count)
+        for far in range(2):
+            @pl.when((parity == far) & (piece >= 0))
+            def _():
+                to_relay(far, piece).wait_recv()
+                forward(far, piece).start()
+
+    def send_first(index):
+        for direction in range(2, 4):
             @pl.when(present[direction])
             def _():
                 send(direction, index).start()
+
+        if not relays:
+            for direction in range(2):
+                @pl.when(present[direction])
+                def _():
+                    send(direction, index).start()
+            return
+
+        for far in range(2):
+            @pl.when((parity == far) & present[far] & (index < out_count))
+            def _():
+                to_relay(far, index).start()
+
+            @pl.when((parity == far) & present[far] & (index >= out_count))
+            def _():
+                send(far, index).start()
+
+            @pl.when((parity == far) & (out_count == 0))
+            def _():
+                send(1 - far, index).start()
+
+    def send_rest():
+        if not relays:
+            return
+        for far in range(2):
+            @pl.when((parity == far) & (out_count > 0))
+            def _():
+                @pl.loop(0, chunks)
+                def _(index):
+                    send(1 - far, index).start()
 
     @pl.loop(0, chunks)
     def _(index):
@@ -197,9 +265,10 @@
     @pl.loop(1, chunks)
     def _(index):
         pack(index)
-        send_all(index - 1)
-
-    send_all(chunks - 1)
+        send_first(index - 1)
+
+    send_first(chunks - 1)
+    send_rest()
 
     for direction in range(4):
         @pl.when(jnp.logical_not(present[direction]))
@@ -223,6 +292,8 @@
 
     @pl.loop(0, chunks)
     def _(index):
+        if relays:
+            pass_on(index)
         fetch(index, p_ref, p_all, p_sem).wait()
         await_halo(2, index)
         await_halo(3, index)
@@ -403,6 +474,14 @@
                 send_sem=send_sem.at[direction], recv_sem=recv_sem.at[direction, 0],
                 device_id=target[direction], device_id_type=pl.DeviceIdType.MESH,
             ).wait_send()
+
+    if relays:
+        for far in range(2):
+            @pl.when(parity == far)
+            def _():
+                @pl.loop(0, relay_count)
+                def _(index):
+                    forward(far, index).wait_send()
 
     others = pltpu.make_async_remote_copy(
         src_ref=board.at[pl.ds(1, devices - 1)], dst_ref=board.at[pl.ds(1, devices - 1)],
@@ -521,6 +600,9 @@
             pltpu.SemaphoreType.DMA,
             pltpu.SemaphoreType.DMA,
             pltpu.SemaphoreType.DMA,
+            halo(columns),
+            pltpu.SemaphoreType.DMA((chunks,)),
+            pltpu.SemaphoreType.DMA((chunks,)),
         ],
         compiler_params=pltpu.CompilerParams(
             collective_id=0, has_side_effects=True, vmem_limit_bytes=60 * 1024 * 1024

time: 66.4 us -> 60.4 us (0.910)
  Pallas kernels: 65.6 us -> 59.7 us
    pallas_call x1, Pallas kernels: 65.6 us -> 59.7 us  [body(): pl.pallas_call(functools.partial(kernel, (rows, columns, steps), chunks),...]
where the time goes in v4:
time: 60.4 us; the launch traced here: 60.2 us
  Pallas kernels  59.7 us (99%)
    pallas_call x1, Pallas kernels, body(): pl.pallas_call(functools.partial(kernel, (rows, columns, steps), chunks),...  59.7 us

profile of v4, /device:TPU:0, one launch (start us, length us, event | category | flops | bytes accessed | tf_op | source)
XLA Modules:
  0.0 60.2 jit_solution(16519104727410981096)
XLA Ops:
  0.0 59.7 %equalise.1 = f32[2,4]{1,0:T(2,128)S(1)} custom-call(s32[2,4,4096,128]{3,2,1,0:T(8,128)} %bitcast.10, bf16[2,4,4096,128]{3,2,1,0:T(8,128)(2,1)} %bitcast.11, s32[2,16,16]{2,1,0:T(8,128)} %adjacency_hbm.1), custom_call_target="tpu_custom_call" | custom-call | tf_op jit(solution)/shard_map/equalise/pallas_call | solution.py:577
  59.7 0.6 copy.7

commit v5 on v4

--- a/solution.py
+++ b/solution.py
@@ -106,7 +106,7 @@
     p_all, w_all, up_out, down_out, left_out, right_out, up_in, down_in, left_in, right_in, sums,
     hist, row_out, column_out, row_in, column_in, tile, board, grid, adjacency_ref,
     p_sem, w_sem, send_sem, recv_sem, near_send, near_recv, far_send, far_recv, adjacency_sem,
-    relay_in, relay_send, relay_recv,
+    relay_in, relay_send, relay_recv, told,
 ):
     rows, columns, steps = shape
     span = steps // chunks
@@ -164,11 +164,35 @@
     def device(index):
         return {"gx": index // y_count, "gy": index % y_count}
 
-    @pl.loop(1, devices)
-    def _(step):
-        pl.semaphore_signal(
-            barrier, inc=1, device_id=device((me + step) % devices), device_id_type=pl.DeviceIdType.MESH
-        )
+    greeted = list(zip(present, target))
+    greeted.append((y_index > 1, {"gx": x_index, "gy": y_index - 2}))
+    greeted.append((y_index < y_count - 2, {"gx": x_index, "gy": y_index + 2}))
+    for here, there in greeted:
+        @pl.when(here)
+        def _():
+            pl.semaphore_signal(barrier, inc=1, device_id=there, device_id_type=pl.DeviceIdType.MESH)
+
+    rounds = -(-(x_count + y_count - 4) // chunks)
+
+    def tell():
+        for direction in range(4):
+            @pl.when(present[direction])
+            def _():
+                pl.semaphore_signal(
+                    told.at[direction ^ 1], inc=1, device_id=target[direction],
+                    device_id_type=pl.DeviceIdType.MESH,
+                )
+
+    def hear():
+        for direction in range(4):
+            @pl.when(present[direction])
+            def _():
+                pl.semaphore_wait(told.at[direction], 1)
+
+    def pass_word():
+        for _ in range(rounds):
+            hear()
+            tell()
 
     def pack(index):
         fetch(index, w_ref, w_all, w_sem).wait()
@@ -260,7 +284,8 @@
     adjacency_copy = pltpu.make_async_copy(adjacency_hbm, adjacency_ref, adjacency_sem)
     adjacency_copy.start()
     pack(0)
-    pl.semaphore_wait(barrier, devices - 1)
+    pl.semaphore_wait(barrier, sum(jnp.where(here, 1, 0) for here, _ in greeted))
+    tell()
 
     @pl.loop(1, chunks)
     def _(index):
@@ -292,6 +317,7 @@
 
     @pl.loop(0, chunks)
     def _(index):
+        pass_word()
         if relays:
             pass_on(index)
         fetch(index, p_ref, p_all, p_sem).wait()
@@ -401,8 +427,11 @@
 
     grid_rows, grid_columns = y_count * rows, x_count * columns
     number_of = {strip: n for n, strips in enumerate(groups) for strip in strips}
-    late = sorted({number_of[strip] for strip in borders[0] + borders[1]})
-    finish([n for n in range(len(groups)) if n not in late])
+    def numbers_of(strips):
+        return sorted({number_of[strip] for strip in strips})
+
+    hear()
+    finish(numbers_of(borders[2]))
     for row in range(rows):
         column_out[row] = hist[place_of((row, 0, 2))]
 
@@ -417,13 +446,16 @@
         edge(0, index)
         edge(1, index)
 
-    finish(late)
+    finish(numbers_of(borders[0]))
     for column in range(columns):
         row_out[column] = hist[place_of((0, column, 0))]
 
     @pl.when(present[0])
     def _():
         near_copy(0).start()
+
+    rest = numbers_of(borders[1] + borders[3])
+    finish(rest + [n for n in range(len(inner))])
 
     @pl.when(present[3])
     def _():
@@ -534,16 +566,22 @@
     def mean_of(values):
         return jnp.sum(jnp.sum(values, axis=0, keepdims=True), axis=1, keepdims=True) / tiles
 
-    def sweep(_, fresh):
-        return (
+    column_sums = (
+        pltpu.roll(up_part, grid_rows - 1, 0) + pltpu.roll(down_part, 1, 0)
+        + pltpu.roll(left_part, lanes - 1, 1) + pltpu.roll(right_part, 1, 1)
+    )
+    push_mean, pull_mean = mean_of(push), mean_of(pull)
+    fresh, mean = push, push_mean
+    for _ in range(ITERS - 1):
+        ahead = mean_of(column_sums * fresh)
+        fresh = (
             up_part * pltpu.roll(fresh, 1, 0)
             + down_part * pltpu.roll(fresh, grid_rows - 1, 0)
             + left_part * pltpu.roll(fresh, 1, 1)
             + right_part * pltpu.roll(fresh, lanes - 1, 1)
             + push
-        ) - pull * mean_of(fresh)
-
-    fresh = lax.fori_loop(0, ITERS - 1, sweep, push)
+        ) - pull * mean
+        mean = ahead + push_mean - pull_mean * mean
     log_gain = fresh - mean_of(fresh)
     result = jnp.zeros((rows, columns), jnp.float32)
     out_row = lax.broadcasted_iota(jnp.int32, (rows, columns), 0)
@@ -603,6 +641,7 @@
             halo(columns),
             pltpu.SemaphoreType.DMA((chunks,)),
             pltpu.SemaphoreType.DMA((chunks,)),
+            pltpu.SemaphoreType.REGULAR((4,)),
         ],
         compiler_params=pltpu.CompilerParams(
             collective_id=0, has_side_effects=True, vmem_limit_bytes=60 * 1024 * 1024

time: 60.4 us -> 59.8 us (0.990)
  no operation moved by 1% of the time
where the time goes in v5:
time: 59.8 us; the launch traced here: 59.7 us
  Pallas kernels  59.1 us (99%)
    pallas_call x1, Pallas kernels, body(): pl.pallas_call(functools.partial(kernel, (rows, columns, steps), chunks),...  59.1 us

profile of v5, /device:TPU:0, one launch (start us, length us, event | category | flops | bytes accessed | tf_op | source)
XLA Modules:
  0.0 59.7 jit_solution(6117673423346632185)
XLA Ops:
  0.0 59.1 %equalise.1 = f32[2,4]{1,0:T(2,128)S(1)} custom-call(s32[2,4,4096,128]{3,2,1,0:T(8,128)} %bitcast.10, bf16[2,4,4096,128]{3,2,1,0:T(8,128)(2,1)} %bitcast.11, s32[2,16,16]{2,1,0:T(8,128)} %adjacency_hbm.1), custom_call_target="tpu_custom_call" | custom-call | tf_op jit(solution)/shard_map/equalise/pallas_call | solution.py:615
  59.1 0.6 copy.7

commit v6 on v5

--- a/solution.py
+++ b/solution.py
@@ -234,9 +234,9 @@
         )
 
     def pass_on(index):
-        piece = index - (chunks - relay_count)
+        piece = index - (chunks - relay_count) + 1
         for far in range(2):
-            @pl.when((parity == far) & (piece >= 0))
+            @pl.when((parity == far) & (piece >= 0) & (piece < relay_count))
             def _():
                 to_relay(far, piece).wait_recv()
                 forward(far, piece).start()
@@ -300,19 +300,24 @@
         def _():
             ins[direction][...] = jnp.zeros_like(ins[direction])
 
-    sums[...] = jnp.zeros_like(sums)
+    def clear(first, count):
+        sums[first : first + count] = jnp.zeros((count, 256, 256), jnp.float32)
+
+    clear(0, len(groups))
+    for number in sorted({groups.index(g) for d in range(2) for g in groups_of(borders[d])}):
+        clear(number + len(groups), 1)
 
     def bins_of(strips, index):
         return flat(gather(p_all, strips, pl.multiple_of(index * height, 16), height, side), jnp.int16)
 
-    def edge(direction, index):
+    def edge(direction, index, spare=0):
         base = index * span * len(borders[direction])
         for strips in groups_of(borders[direction]):
             length = height * len(strips) // 4
             window = pl.ds(pl.multiple_of(base, 16), length)
             mine = outs[direction][window, :].astype(jnp.float32)
             joint = (mine * ins[direction][window, :].astype(jnp.float32)).astype(jnp.bfloat16)
-            sums[groups.index(strips)] += outer_product(bins_of(strips, index), joint)
+            sums[groups.index(strips) + spare * len(groups)] += outer_product(bins_of(strips, index), joint)
             base += length
 
     @pl.loop(0, chunks)
@@ -345,12 +350,23 @@
             device_id=where, device_id_type=pl.DeviceIdType.MESH,
         )
 
+    grid_rows, grid_columns = y_count * rows, x_count * columns
+    number_of = {strip: n for n, strips in enumerate(groups) for strip in strips}
+    def numbers_of(strips):
+        return sorted({number_of[strip] for strip in strips})
+
+    pair = 2 if chunks % 2 == 0 else 1
+
     def finish(numbers):
         a = lax.broadcasted_iota(jnp.int32, (256, 256), 0)
         b = lax.broadcasted_iota(jnp.int32, (256, 256), 1)
+        halves = numbers_of(borders[0] + borders[1]) if pair == 2 else []
         packed = []
         for number in numbers:
-            kept = jnp.where(a % 16 == b % 16, sums[number], 0.0)
+            total = sums[number]
+            if number in halves:
+                total += sums[number + len(groups)]
+            kept = jnp.where(a % 16 == b % 16, total, 0.0)
             packed.append(jnp.sum(kept.reshape(16, 16, 256), axis=1))
         packed = jnp.concatenate(packed, axis=0)
         lane = lax.broadcasted_iota(jnp.int32, (256, 64), 0)
@@ -425,11 +441,6 @@
             )
         return lines
 
-    grid_rows, grid_columns = y_count * rows, x_count * columns
-    number_of = {strip: n for n, strips in enumerate(groups) for strip in strips}
-    def numbers_of(strips):
-        return sorted({number_of[strip] for strip in strips})
-
     hear()
     finish(numbers_of(borders[2]))
     for row in range(rows):
@@ -439,20 +450,34 @@
     def _():
         near_copy(1).start()
 
-    @pl.loop(0, chunks)
-    def _(index):
-        await_halo(0, index)
-        await_halo(1, index)
-        edge(0, index)
-        edge(1, index)
-
-    finish(numbers_of(borders[0]))
-    for column in range(columns):
-        row_out[column] = hist[place_of((0, column, 0))]
-
-    @pl.when(present[0])
+    def border_pass(direction):
+        @pl.loop(0, chunks // pair)
+        def _(index):
+            for spare in range(pair):
+                await_halo(direction, index * pair + spare)
+            for spare in range(pair):
+                edge(direction, index * pair + spare, spare)
+
+    def send_up_sums():
+        finish(numbers_of(borders[0]))
+        for column in range(columns):
+            row_out[column] = hist[place_of((0, column, 0))]
+
+        @pl.when(present[0])
+        def _():
+            near_copy(0).start()
+
+    @pl.when(parity == 0)
     def _():
-        near_copy(0).start()
+        border_pass(0)
+        send_up_sums()
+        border_pass(1)
+
+    @pl.when(parity == 1)
+    def _():
+        border_pass(1)
+        border_pass(0)
+        send_up_sums()
 
     rest = numbers_of(borders[1] + borders[3])
     finish(rest + [n for n in range(len(inner))])
@@ -622,7 +647,7 @@
             pltpu.VMEM((rows, columns, steps * sides, 128), jnp.bfloat16),
             *halos,
             *halos,
-            pltpu.VMEM((len(all_groups(rows, columns)), 256, 256), jnp.float32),
+            pltpu.VMEM((2 * len(all_groups(rows, columns)), 256, 256), jnp.float32),
             pltpu.VMEM((rows * columns * sides, 16, 16), jnp.float32),
             *([pltpu.VMEM((columns, 16, 16), jnp.float32), pltpu.VMEM((rows, 16, 16), jnp.float32)] * 2),
             pltpu.VMEM((rows, lanes), jnp.float32),

time: 59.8 us -> 58.8 us (0.983)
  Pallas kernels: 59.1 us -> 58.1 us
    pallas_call x1, Pallas kernels: 59.1 us -> 58.1 us  [body(): pl.pallas_call(functools.partial(kernel, (rows, columns, steps), chunks),...]
where the time goes in v6:
time: 58.8 us; the launch traced here: 58.6 us
  Pallas kernels  58.1 us (99%)
    pallas_call x1, Pallas kernels, body(): pl.pallas_call(functools.partial(kernel, (rows, columns, steps), chunks),...  58.1 us

profile of v6, /device:TPU:0, one launch (start us, length us, event | category | flops | bytes accessed | tf_op | source)
XLA Modules:
  0.0 58.6 jit_solution(3923159376907979774)
XLA Ops:
  0.0 58.1 %equalise.1 = f32[2,4]{1,0:T(2,128)S(1)} custom-call(s32[2,4,4096,128]{3,2,1,0:T(8,128)} %bitcast.10, bf16[2,4,4096,128]{3,2,1,0:T(8,128)(2,1)} %bitcast.11, s32[2,16,16]{2,1,0:T(8,128)} %adjacency_hbm.1), custom_call_target="tpu_custom_call" | custom-call | tf_op jit(solution)/shard_map/equalise/pallas_call | solution.py:640
  58.1 0.6 copy.7

commit v7 on v6

--- a/solution.py
+++ b/solution.py
@@ -283,6 +283,18 @@
 
     adjacency_copy = pltpu.make_async_copy(adjacency_hbm, adjacency_ref, adjacency_sem)
     adjacency_copy.start()
+    for direction in range(4):
+        @pl.when(jnp.logical_not(present[direction]))
+        def _():
+            ins[direction][...] = jnp.zeros_like(ins[direction])
+
+    def clear(first, count):
+        sums[first : first + count] = jnp.zeros((count, 256, 256), jnp.float32)
+
+    clear(0, len(groups))
+    for number in sorted({groups.index(g) for d in range(2) for g in groups_of(borders[d])}):
+        clear(number + len(groups), 1)
+
     pack(0)
     pl.semaphore_wait(barrier, sum(jnp.where(here, 1, 0) for here, _ in greeted))
     tell()
@@ -295,29 +307,21 @@
     send_first(chunks - 1)
     send_rest()
 
-    for direction in range(4):
-        @pl.when(jnp.logical_not(present[direction]))
-        def _():
-            ins[direction][...] = jnp.zeros_like(ins[direction])
-
-    def clear(first, count):
-        sums[first : first + count] = jnp.zeros((count, 256, 256), jnp.float32)
-
-    clear(0, len(groups))
-    for number in sorted({groups.index(g) for d in range(2) for g in groups_of(borders[d])}):
-        clear(number + len(groups), 1)
-
     def bins_of(strips, index):
         return flat(gather(p_all, strips, pl.multiple_of(index * height, 16), height, side), jnp.int16)
 
-    def edge(direction, index, spare=0):
+    def edge(direction, index, spare=0, split=1):
         base = index * span * len(borders[direction])
         for strips in groups_of(borders[direction]):
             length = height * len(strips) // 4
             window = pl.ds(pl.multiple_of(base, 16), length)
             mine = outs[direction][window, :].astype(jnp.float32)
             joint = (mine * ins[direction][window, :].astype(jnp.float32)).astype(jnp.bfloat16)
-            sums[groups.index(strips) + spare * len(groups)] += outer_product(bins_of(strips, index), joint)
+            bins, piece = bins_of(strips, index), length // split
+            for number in range(split):
+                part = slice(number * piece, number * piece + piece)
+                place = groups.index(strips) + (spare + number) * len(groups)
+                sums[place] += outer_product(bins[part], joint[part])
             base += length
 
     @pl.loop(0, chunks)
@@ -450,14 +454,21 @@
     def _():
         near_copy(1).start()
 
-    def border_pass(direction):
-        @pl.loop(0, chunks // pair)
+    def border_pass(direction, last):
+        apart = last and pair == 2 and span % 32 == 0
+
+        @pl.loop(0, chunks // pair - apart)
         def _(index):
             for spare in range(pair):
                 await_halo(direction, index * pair + spare)
             for spare in range(pair):
                 edge(direction, index * pair + spare, spare)
 
+        if apart:
+            for index in range(chunks - 2, chunks):
+                await_halo(direction, index)
+                edge(direction, index, split=2)
+
     def send_up_sums():
         finish(numbers_of(borders[0]))
         for column in range(columns):
@@ -469,14 +480,14 @@
 
     @pl.when(parity == 0)
     def _():
-        border_pass(0)
+        border_pass(0, False)
         send_up_sums()
-        border_pass(1)
+        border_pass(1, True)
 
     @pl.when(parity == 1)
     def _():
-        border_pass(1)
-        border_pass(0)
+        border_pass(1, False)
+        border_pass(0, True)
         send_up_sums()
 
     rest = numbers_of(borders[1] + borders[3])
@@ -514,9 +525,15 @@
             device_id=device(index), device_id_type=pl.DeviceIdType.MESH,
         )
 
-    @pl.loop(1, devices)
+    @pl.loop(0, devices)
     def _(step):
-        spread((me + step) % devices, me).start()
+        line = step // x_count
+        farthest = jnp.where(2 * y_index < y_count, y_count - 1 - line, line)
+        index = (step % x_count) * y_count + farthest
+
+        @pl.when(index != me)
+        def _():
+            spread(index, me).start()
 
     for number in range(2):
         @pl.when(present[2 * number])

time: 58.8 us -> 58.3 us (level)
  no operation moved by 1% of the time
where the time goes in v7:
time: 58.3 us; the launch traced here: 58.1 us
  Pallas kernels  57.6 us (99%)
    pallas_call x1, Pallas kernels, body(): pl.pallas_call(functools.partial(kernel, (rows, columns, steps), chunks),...  57.6 us

profile of v7, /device:TPU:0, one launch (start us, length us, event | category | flops | bytes accessed | tf_op | source)
XLA Modules:
  0.0 58.1 jit_solution(6525797991045115014)
XLA Ops:
  0.0 57.6 %equalise.1 = f32[2,4]{1,0:T(2,128)S(1)} custom-call(s32[2,4,4096,128]{3,2,1,0:T(8,128)} %bitcast.10, bf16[2,4,4096,128]{3,2,1,0:T(8,128)(2,1)} %bitcast.11, s32[2,16,16]{2,1,0:T(8,128)} %adjacency_hbm.1), custom_call_target="tpu_custom_call" | custom-call | tf_op jit(solution)/shard_map/equalise/pallas_call | solution.py:657
  57.6 0.6 copy.7
